TPU v7x, 32 devices: a whole 2x2x4 slice. The times are simulated.
32 devices in a mesh: seq: 8 (over z, x), head: 4 (over y, core).
Axes of the slice: x: 2, y: 2, z: 4, core: 2. Of those that a mesh axis runs over, the one named last changes fastest.
Arguments:
- block_input: bfloat16 [4096, 2048], P('seq'), may hold values from -6 to 6
- out_cotangent: bfloat16 [4096, 2048], P('seq'), may hold values from -6 to 6
- decay_rate: float32 [8], P('head'), may hold values from 0 to 1, as said below
- first_scale: float32 [2048], replicated, may hold values from 0.5 to 1.5
- first_shift: float32 [2048], replicated, may hold values from -3 to 3
- query_weight: bfloat16 [2048, 2048], P(None, 'head'), may hold values from -0.125 to 0.125
- key_weight: bfloat16 [2048, 2048], P(None, 'head'), may hold values from -0.125 to 0.125
- value_weight: bfloat16 [2048, 4096], P(None, 'head'), may hold values from -0.125 to 0.125
- gate_weight: bfloat16 [2048, 4096], P(None, 'head'), may hold values from -0.125 to 0.125
- output_weight: bfloat16 [4096, 2048], P('head'), may hold values from -0.1875 to 0.1875
- second_scale: float32 [2048], replicated, may hold values from 0.5 to 1.5
- second_shift: float32 [2048], replicated, may hold values from -3 to 3
- up_weight: bfloat16 [2048, 4096], P(None, 'head'), may hold values from -0.125 to 0.125
- mlp_gate_weight: bfloat16 [2048, 4096], P(None, 'head'), may hold values from -0.125 to 0.125
- down_weight: bfloat16 [4096, 2048], P('head'), may hold values from -0.1875 to 0.1875
Outputs:
- block_output: bfloat16 [4096, 2048], P('seq')
- input_grad: bfloat16 [4096, 2048], P('seq')
- first_scale_grad: float32 [2048], P('seq')
- first_shift_grad: float32 [2048], P('seq')
- query_grad: float32 [2048, 2048], P('seq', 'head')
- key_grad: float32 [2048, 2048], P('seq', 'head')
- value_grad: float32 [2048, 4096], P('seq', 'head')
- gate_grad: float32 [2048, 4096], P('seq', 'head')
- output_grad: float32 [4096, 2048], P('head', 'seq')
- second_scale_grad: float32 [2048], P('seq')
- second_shift_grad: float32 [2048], P('seq')
- up_grad: float32 [2048, 4096], P('seq', 'head')
- mlp_gate_grad: float32 [2048, 4096], P('seq', 'head')
- down_grad: float32 [4096, 2048], P('head', 'seq')
Inputs may be any that keep to these rules, and one draw needn't show every extreme that they name: `decay_rate`: every rate is positive.
All inputs are finite; a program needn't handle non-finite values.
Results may differ from a plain program's by a relative error of at most 0.015.
The roundings to bfloat16 on the way count: a program that leaves them out, or rounds other values in their place, can miss the bound.
Values sent between devices are 32-bit elements; how exact they have to be, the bound alone decides.
A program may use at most 256 MiB of HBM per device.

v0:
```python
import jax
import jax.numpy as jnp
from jax import lax
from jax.sharding import PartitionSpec as P

KD = 256
VD = 512


EPSILON = 1e-05
FULL_ACCURACY = lax.Precision.HIGHEST


def entering(x, axis, combine, identity, reverse):
    count, position = (lax.axis_size(axis), lax.axis_index(axis))
    everything = jax.tree.map(lambda part: lax.all_gather(part, axis), x)
    start = jax.tree.map(
        lambda part, zero: jnp.broadcast_to(jnp.asarray(zero, part.dtype), part.shape), x, identity
    )

    def lap(k, before):
        at = count - 1 - k if reverse else k
        reached = at > position if reverse else at < position
        new = combine(before, jax.tree.map(lambda part: part[at], everything))
        return jax.tree.map(lambda a, b: jnp.where(reached, a, b), new, before)

    return lax.fori_loop(0, count, lap, start)


def layer_norm(values, scales, shifts):
    centred = values - jnp.mean(values, axis=-1, keepdims=True)
    inverse = lax.rsqrt(jnp.mean(centred * centred, axis=-1, keepdims=True) + EPSILON)
    normed = centred * inverse
    return (normed * scales + shifts, normed, inverse)


def norm_back(upstream, normed, inverse):
    return inverse * (
        upstream
        - jnp.mean(upstream, axis=-1, keepdims=True)
        - normed * jnp.mean(upstream * normed, axis=-1, keepdims=True)
    )


def gelu_pair(pre_act):
    normal_cdf = 0.5 * (1.0 + lax.erf(pre_act * 0.7071067811865476))
    density = jnp.exp(-0.5 * pre_act * pre_act) * 0.3989422804014327
    return (pre_act * normal_cdf, normal_cdf + pre_act * density)


def decay_tables(decay_rates, length):
    places = jnp.arange(length, dtype=jnp.float32)
    distance = places[:, None] - places[None, :]
    causal = distance >= 0.0
    decay_mask = jnp.where(
        causal[None],
        jnp.exp(-decay_rates[:, None, None] * jnp.where(causal, distance, 0.0)[None]),
        0.0,
    )
    arriving_fading_factor = jnp.exp(-places[:, None] * decay_rates[None, :])[:, :, None]
    outgoing_decay = jnp.exp(-(length - places)[:, None] * decay_rates[None, :])[:, :, None]
    return (decay_mask, arriving_fading_factor, outgoing_decay)


def contract_rows(left_side, right_side):
    return lax.dot_general(
        left_side, right_side, (((0,), (0,)), ((), ())), preferred_element_type=jnp.float32
    )


def times_transpose(left_side, right_side):
    return lax.dot_general(
        left_side, right_side, (((1,), (1,)), ((), ())), preferred_element_type=jnp.float32
    )


def chain_step(earlier_part, later_part):
    return (
        earlier_part[0] * later_part[0],
        later_part[0][:, None, None] * earlier_part[1] + later_part[1],
    )


def shards(
    block_input,
    out_cotangent,
    decay_rate,
    first_scale,
    first_shift,
    query_weight,
    key_weight,
    value_weight,
    gate_weight,
    output_weight,
    second_scale,
    second_shift,
    up_weight,
    mlp_gate_weight,
    down_weight,
):
    length = block_input.shape[0]
    local_heads = decay_rate.shape[0]
    decay_mask, arriving_fading_factor, outgoing_decay = decay_tables(decay_rate, length)
    block_decay = jnp.exp(-decay_rate * length)
    inputs = block_input.astype(jnp.float32)
    first_out, first_normed, first_inverse = layer_norm(inputs, first_scale, first_shift)
    first_act = first_out.astype(jnp.bfloat16)
    queries = jnp.dot(first_act, query_weight, preferred_element_type=jnp.float32).astype(
        jnp.bfloat16
    )
    key_rows = jnp.dot(first_act, key_weight, preferred_element_type=jnp.float32).astype(
        jnp.bfloat16
    )
    value_rows = jnp.dot(first_act, value_weight, preferred_element_type=jnp.float32).astype(
        jnp.bfloat16
    )
    gate_pre = jnp.dot(first_act, gate_weight, preferred_element_type=jnp.float32)
    query_heads = queries.reshape(length, local_heads, KD)
    key_heads = key_rows.reshape(length, local_heads, KD)
    value_heads = value_rows.reshape(length, local_heads, VD)
    probe_broadcast = query_heads.astype(jnp.float32)
    key_expanded = key_heads.astype(jnp.float32)
    value_expanded = value_heads.astype(jnp.float32)
    block_local_state = jnp.einsum(
        "xue,xuz->uez", key_expanded * outgoing_decay, value_expanded, precision=FULL_ACCURACY
    )
    identity = (jnp.ones_like(block_decay), jnp.zeros_like(block_local_state))
    prefix_decay, arriving_memory_matrix = entering(
        (block_decay, block_local_state), "seq", chain_step, identity, False
    )
    scores = (
        jnp.einsum("ihk,jhk->hij", query_heads, key_heads, preferred_element_type=jnp.float32)
        * decay_mask
    )
    retain_weights = scores.astype(jnp.bfloat16)
    intra_segment_term = jnp.einsum(
        "hij,jhv->ihv", retain_weights, value_heads, preferred_element_type=jnp.float32
    )
    memory_mixer_result = intra_segment_term + arriving_fading_factor * jnp.einsum(
        "qtj,tjz->qtz", probe_broadcast, arriving_memory_matrix, precision=FULL_ACCURACY
    )
    group_centred = memory_mixer_result - jnp.mean(memory_mixer_result, axis=-1, keepdims=True)
    cluster_reciprocal_spread = lax.rsqrt(
        jnp.mean(group_centred * group_centred, axis=-1, keepdims=True) + EPSILON
    )
    group_normed = group_centred * cluster_reciprocal_spread
    sigmoid_gate = jax.nn.sigmoid(gate_pre)
    swish_gate = gate_pre * sigmoid_gate
    group_flat = group_normed.reshape(length, local_heads * VD)
    gated_rows = (swish_gate * group_flat).astype(jnp.bfloat16)
    mixer_out = lax.psum(
        jnp.dot(gated_rows, output_weight, preferred_element_type=jnp.float32), "head"
    )
    hidden_state = inputs + mixer_out
    second_out, second_normed, second_inverse = layer_norm(hidden_state, second_scale, second_shift)
    second_act = second_out.astype(jnp.bfloat16)
    up_pre = jnp.dot(second_act, up_weight, preferred_element_type=jnp.float32)
    mlp_pre = jnp.dot(second_act, mlp_gate_weight, preferred_element_type=jnp.float32)
    gelu_value, gelu_slope = gelu_pair(mlp_pre)
    product = (gelu_value * up_pre).astype(jnp.bfloat16)
    mlp_out = lax.psum(jnp.dot(product, down_weight, preferred_element_type=jnp.float32), "head")
    block_output = (hidden_state + mlp_out).astype(jnp.bfloat16)
    cotangent = out_cotangent.astype(jnp.float32)
    down_grad = contract_rows(product, out_cotangent)
    product_grad = times_transpose(out_cotangent, down_weight)
    up_pre_grad = (product_grad * gelu_value).astype(jnp.bfloat16)
    mlp_pre_grad = (product_grad * up_pre * gelu_slope).astype(jnp.bfloat16)
    up_grad = contract_rows(second_act, up_pre_grad)
    mlp_gate_grad = contract_rows(second_act, mlp_pre_grad)
    second_act_grad = lax.psum(
        times_transpose(up_pre_grad, up_weight) + times_transpose(mlp_pre_grad, mlp_gate_weight),
        "head",
    )
    second_scale_grad = jnp.sum(second_act_grad * second_normed, axis=0)
    second_shift_grad = jnp.sum(second_act_grad, axis=0)
    hidden_grad = cotangent + norm_back(
        second_act_grad * second_scale, second_normed, second_inverse
    )
    hidden_cast = hidden_grad.astype(jnp.bfloat16)
    output_grad = contract_rows(gated_rows, hidden_cast)
    gated_grad = times_transpose(hidden_cast, output_weight)
    gate_pre_grad = (
        gated_grad * group_flat * sigmoid_gate * (1.0 + gate_pre * (1.0 - sigmoid_gate))
    ).astype(jnp.bfloat16)
    normed_grad = (gated_grad * swish_gate).reshape(length, local_heads, VD)
    retained_grad = norm_back(normed_grad, group_normed, cluster_reciprocal_spread).astype(
        jnp.bfloat16
    )
    memory_mixer_result_broadcast = retained_grad.astype(jnp.float32)
    state_contribution = jnp.einsum(
        "gdt,gdc->dtc",
        probe_broadcast * arriving_fading_factor,
        memory_mixer_result_broadcast,
        precision=FULL_ACCURACY,
    )
    suffix_decay, state_gradient = entering(
        (block_decay, state_contribution), "seq", chain_step, identity, True
    )
    score_grad = (
        jnp.einsum("ihv,jhv->hij", retained_grad, value_heads, preferred_element_type=jnp.float32)
        * decay_mask
    ).astype(jnp.bfloat16)
    query_heads_gradient = (
        jnp.einsum("uwa,auc->wuc", score_grad, key_heads, preferred_element_type=jnp.float32)
        + arriving_fading_factor
        * jnp.einsum(
            "xzu,zwu->xzw",
            memory_mixer_result_broadcast,
            arriving_memory_matrix,
            precision=FULL_ACCURACY,
        )
    ).astype(jnp.bfloat16)
    key_heads_gradient = (
        jnp.einsum("eus,ueg->seg", score_grad, query_heads, preferred_element_type=jnp.float32)
        + outgoing_decay
        * jnp.einsum("xwm,wlm->xwl", value_expanded, state_gradient, precision=FULL_ACCURACY)
    ).astype(jnp.bfloat16)
    value_heads_gradient = (
        jnp.einsum(
            "npl,pnw->lnw", retain_weights, retained_grad, preferred_element_type=jnp.float32
        )
        + outgoing_decay
        * jnp.einsum("wra,rag->wrg", key_expanded, state_gradient, precision=FULL_ACCURACY)
    ).astype(jnp.bfloat16)
    query_flat = query_heads_gradient.reshape(length, local_heads * KD)
    key_flat = key_heads_gradient.reshape(length, local_heads * KD)
    value_flat = value_heads_gradient.reshape(length, local_heads * VD)
    query_grad = contract_rows(first_act, query_flat)
    key_grad = contract_rows(first_act, key_flat)
    value_grad = contract_rows(first_act, value_flat)
    gate_grad = contract_rows(first_act, gate_pre_grad)
    first_act_grad = lax.psum(
        times_transpose(query_flat, query_weight)
        + times_transpose(key_flat, key_weight)
        + times_transpose(value_flat, value_weight)
        + times_transpose(gate_pre_grad, gate_weight),
        "head",
    )
    first_scale_grad = jnp.sum(first_act_grad * first_normed, axis=0)
    first_shift_grad = jnp.sum(first_act_grad, axis=0)
    input_grad = (
        hidden_grad + norm_back(first_act_grad * first_scale, first_normed, first_inverse)
    ).astype(jnp.bfloat16)
    summed = (
        lax.psum_scatter(first_scale_grad, "seq", scatter_dimension=0, tiled=True),
        lax.psum_scatter(first_shift_grad, "seq", scatter_dimension=0, tiled=True),
        lax.psum_scatter(query_grad, "seq", scatter_dimension=0, tiled=True),
        lax.psum_scatter(key_grad, "seq", scatter_dimension=0, tiled=True),
        lax.psum_scatter(value_grad, "seq", scatter_dimension=0, tiled=True),
        lax.psum_scatter(gate_grad, "seq", scatter_dimension=0, tiled=True),
        lax.psum_scatter(output_grad, "seq", scatter_dimension=1, tiled=True),
        lax.psum_scatter(second_scale_grad, "seq", scatter_dimension=0, tiled=True),
        lax.psum_scatter(second_shift_grad, "seq", scatter_dimension=0, tiled=True),
        lax.psum_scatter(up_grad, "seq", scatter_dimension=0, tiled=True),
        lax.psum_scatter(mlp_gate_grad, "seq", scatter_dimension=0, tiled=True),
        lax.psum_scatter(down_grad, "seq", scatter_dimension=1, tiled=True),
    )
    return (
        block_output,
        input_grad,
        summed[0],
        summed[1],
        summed[2],
        summed[3],
        summed[4],
        summed[5],
        summed[6],
        summed[7],
        summed[8],
        summed[9],
        summed[10],
        summed[11],
    )


def solution(mesh):
    in_specs = (
        P("seq", None),
        P("seq", None),
        P("head"),
        P(),
        P(),
        P(None, "head"),
        P(None, "head"),
        P(None, "head"),
        P(None, "head"),
        P("head", None),
        P(),
        P(),
        P(None, "head"),
        P(None, "head"),
        P("head", None),
    )
    out_specs = (
        P("seq", None),
        P("seq", None),
        P("seq"),
        P("seq"),
        P("seq", "head"),
        P("seq", "head"),
        P("seq", "head"),
        P("seq", "head"),
        P("head", "seq"),
        P("seq"),
        P("seq"),
        P("seq", "head"),
        P("seq", "head"),
        P("head", "seq"),
    )
    return jax.shard_map(shards, mesh=mesh, in_specs=in_specs, out_specs=out_specs, check_vma=False)
```

profile of v0, /device:TPU:0, one launch (start us, length us, event | category | flops | bytes accessed | tf_op | source)
XLA Modules:
  0.0 1808.1 jit_solution(9808282014992432621)
XLA Ops:
  21.6 24.1 %all-reduce = f32[16]{0:T(128)S(1)} all-reduce(f32[16]{0:T(128)S(1)} %get-tuple-element.323), channel_id=2, replica_groups=mesh['seq'=8,'head'=4] {'seq'}, use_global_device_ids=true, to_apply=%add | all-reduce | flops 16 | bytes 128
  53.6 94.0 %all-gather.6.cloned.1.call-done = f32[16,256,512]{2,1,0:T(8,128)} async-done(((f32[2,256,512]{2,1,0:T(8,128)}), f32[16,256,512]{2,1,0:T(8,128)}) %all-gather.6.cloned.1.call-update) | async-done | bytes 8388624 | tf_op jit(solution)/shard_map/all_gather | solution.py:16
  147.6 13.2 while.30
  169.2 7.4 multiply_convert_fusion.5
  177.6 4.4 fusion.60
  182.3 6.5 fusion.63
  188.8 77.0 %all-reduce.11.cloned.1.call-done = f32[512,2048]{1,0:T(8,128)} async-done(((f32[512,2048]{1,0:T(8,128)}), f32[512,2048]{1,0:T(8,128)}) %all-reduce.11.cloned.1.call-update) | async-done | bytes 4194320 | tf_op jit(solution)/shard_map/psum | solution.py:151
  283.8 4.4 convolution_add_fusion
  288.7 85.3 %all-reduce.13.cloned.1.call-done = f32[512,2048]{1,0:T(8,128)} async-done(((f32[512,2048]{1,0:T(8,128)}), f32[512,2048]{1,0:T(8,128)}) %all-reduce.13.cloned.1.call-update) | async-done | bytes 4194320 | tf_op jit(solution)/shard_map/psum | solution.py:170
  374.0 4.8 multiply_reduce_fusion
  384.0 4.6 fusion.56
  408.0 7.0 fusion.62
  424.6 4.4 fusion.68
  429.0 103.5 %all-gather.8.cloned.1.call-done = f32[16,256,512]{2,1,0:T(8,128)} async-done(((f32[2,256,512]{2,1,0:T(8,128)}), f32[16,256,512]{2,1,0:T(8,128)}) %all-gather.8.cloned.1.call-update) | async-done | bytes 8388624 | tf_op jit(solution)/shard_map/all_gather | solution.py:16
  532.5 13.6 while.31
  565.1 7.3 fusion.73
  573.6 7.2 fusion.74
  582.0 7.3 fusion.75
  590.6 8.1 fusion.42
  599.9 5.6 fusion.72
  611.1 5.6 fusion.71
  617.5 92.6 %all-reduce.15.cloned.1.call-done = (f32[512,2048]{1,0:T(8,128)}, f32[512,2048]{1,0:T(8,128)}) async-done(((f32[512,2048]{1,0:T(8,128)}, f32[512,2048]{1,0:T(8,128)}), (f32[512,2048]{1,0:T(8,128)}, f32[512,2048]{1,0:T(8,128)})) %all-reduce.15.cloned.1.call-update) | async-done | bytes 8388624 | tf_op jit(solution)/shard_map/psum | solution.py:161
  713.8 38.6 %all-reduce.5 = (f32[2048]{0:T(1024)S(1)}, f32[2048]{0:T(1024)S(1)}, f32[2048]{0:T(1024)S(1)}, f32[2048]{0:T(1024)S(1)}) all-reduce(f32[2048]{0:T(1024)S(1)} %get-tuple-element.280, f32[2048]{0:T(1024)S(1)} %get-tuple-element.285, f32[2048]{0:T(1024)S(1)} %get-tuple-element.278, ...), channel_id=5, replica_groups=mesh['seq'=8,'head'=4] {'seq'}, use_global_device_ids=true, to_apply=%region_21.22.clone | all-reduce | flops 8192 | bytes 65536
  754.9 5.7 add_convert_fusion
  765.2 38.0 %reduce-scatter.9.cloned.1.call-done = f32[256,512]{1,0:T(8,128)} async-done(((f32[2048,512]{1,0:T(8,128)}), f32[256,512]{1,0:T(8,128)}) %reduce-scatter.9.cloned.1.call-update) | async-done | bytes 524304 | tf_op jit(solution)/shard_map/reduce_scatter | solution.py:247
  803.1 151.3 %reduce-scatter.19.cloned.1.call-done = f32[256,1024]{1,0:T(8,128)} async-done(((f32[2048,1024]{1,0:T(8,128)}), f32[256,1024]{1,0:T(8,128)}) %reduce-scatter.19.cloned.1.call-update) | async-done | bytes 1048592 | tf_op jit(solution)/shard_map/reduce_scatter | solution.py:254
  954.5 150.8 %reduce-scatter.21.cloned.1.call-done = f32[256,1024]{1,0:T(8,128)} async-done(((f32[2048,1024]{1,0:T(8,128)}), f32[256,1024]{1,0:T(8,128)}) %reduce-scatter.21.cloned.1.call-update) | async-done | bytes 1048592 | tf_op jit(solution)/shard_map/reduce_scatter | solution.py:255
  1105.3 151.2 %reduce-scatter.23.cloned.1.call-done = f32[1024,256]{1,0:T(8,128)} async-done(((f32[1024,2048]{1,0:T(8,128)}), f32[1024,256]{1,0:T(8,128)}) %reduce-scatter.23.cloned.1.call-update) | async-done | bytes 1048592 | tf_op jit(solution)/shard_map/reduce_scatter | solution.py:256
  1256.4 151.0 %reduce-scatter.17.cloned.1.call-done = f32[1024,256]{1,0:T(8,128)} async-done(((f32[1024,2048]{1,0:T(8,128)}), f32[1024,256]{1,0:T(8,128)}) %reduce-scatter.17.cloned.1.call-update) | async-done | bytes 1048592 | tf_op jit(solution)/shard_map/reduce_scatter | solution.py:251
  1407.5 150.8 %reduce-scatter.15.cloned.1.call-done = f32[256,1024]{1,0:T(8,128)} async-done(((f32[2048,1024]{1,0:T(8,128)}), f32[256,1024]{1,0:T(8,128)}) %reduce-scatter.15.cloned.1.call-update) | async-done | bytes 1048592 | tf_op jit(solution)/shard_map/reduce_scatter | solution.py:250
  1558.3 91.5 %reduce-scatter.11.cloned.1.call-done = f32[256,512]{1,0:T(8,128)} async-done(((f32[2048,512]{1,0:T(8,128)}), f32[256,512]{1,0:T(8,128)}) %reduce-scatter.11.cloned.1.call-update) | async-done | bytes 524304 | tf_op jit(solution)/shard_map/reduce_scatter | solution.py:248
  1649.7 151.3 %reduce-scatter.13.cloned.1.call-done = f32[256,1024]{1,0:T(8,128)} async-done(((f32[2048,1024]{1,0:T(8,128)}), f32[256,1024]{1,0:T(8,128)}) %reduce-scatter.13.cloned.1.call-update) | async-done | bytes 1048592 | tf_op jit(solution)/shard_map/reduce_scatter | solution.py:249
  (275 shorter events, 149.3 us)
Async XLA Ops:
  7.2 39.0 %copy-start = (bf16[2048,512]{1,0:T(8,128)(2,1)S(1)}, bf16[2048,512]{1,0:T(8,128)(2,1)}, u32[]{:S(2)}) copy-start(bf16[2048,512]{1,0:T(8,128)(2,1)} %param.24) | copy-start | bytes 6291460
  7.2 140.4 %all-gather.6.cloned.1.call-start = ((), (), s32[]{:S(2)}) async-start(), calls=%async_computation.18 | async-start | bytes 9437184 | tf_op jit(solution)/shard_map/all_gather | solution.py:16
  20.2 245.6 %all-reduce.11.cloned.1.call-start = ((), (), s32[]{:S(2)}) async-start(), calls=%async_computation.8 | async-start | bytes 8388608 | tf_op jit(solution)/shard_map/psum | solution.py:151
  169.1 8.4 copy-start.61
  182.0 192.0 %all-reduce.13.cloned.1.call-start = ((), (), s32[]{:S(2)}) async-start(), calls=%async_computation.9 | async-start | bytes 8388608 | tf_op jit(solution)/shard_map/psum | solution.py:170
  288.2 244.3 %all-gather.8.cloned.1.call-start = ((), (), s32[]{:S(2)}) async-start(), calls=%async_computation.19 | async-start | bytes 9437184 | tf_op jit(solution)/shard_map/all_gather | solution.py:16
  374.0 4.9 copy-start.3
  374.0 5.9 copy-start.18
  379.9 4.1 copy-start.74
  383.2 5.4 copy-start.10
  407.8 302.4 %all-reduce.15.cloned.1.call-start = ((), (), s32[]{:S(2)}) async-start(), calls=%async_computation.20 | async-start | bytes 16777216 | tf_op jit(solution)/shard_map/psum | solution.py:161
  408.0 7.0 copy-start.17
  408.0 7.0 copy-start.21
  408.0 7.0 copy-start.43
  532.5 13.6 copy-start.22
  548.6 5.2 copy-start.26
  558.9 244.3 %reduce-scatter.9.cloned.1.call-start = ((), (), s32[]{:S(2)}) async-start(), calls=%async_computation.10 | async-start | bytes 4718592 | tf_op jit(solution)/shard_map/reduce_scatter | solution.py:247
  563.9 390.6 %reduce-scatter.19.cloned.1.call-start = ((), (), s32[]{:S(2)}) async-start(), calls=%async_computation.15 | async-start | bytes 9437184 | tf_op jit(solution)/shard_map/reduce_scatter | solution.py:254
  572.4 532.9 %reduce-scatter.21.cloned.1.call-start = ((), (), s32[]{:S(2)}) async-start(), calls=%async_computation.16 | async-start | bytes 9437184 | tf_op jit(solution)/shard_map/reduce_scatter | solution.py:255
  580.8 675.6 %reduce-scatter.23.cloned.1.call-start = ((), (), s32[]{:S(2)}) async-start(), calls=%async_computation.17 | async-start | bytes 9437184 | tf_op jit(solution)/shard_map/reduce_scatter | solution.py:256
  589.4 818.1 %reduce-scatter.17.cloned.1.call-start = ((), (), s32[]{:S(2)}) async-start(), calls=%async_computation.14 | async-start | bytes 9437184 | tf_op jit(solution)/shard_map/reduce_scatter | solution.py:251
  598.7 959.6 %reduce-scatter.15.cloned.1.call-start = ((), (), s32[]{:S(2)}) async-start(), calls=%async_computation.13 | async-start | bytes 9437184 | tf_op jit(solution)/shard_map/reduce_scatter | solution.py:250
  605.5 1044.2 %reduce-scatter.11.cloned.1.call-start = ((), (), s32[]{:S(2)}) async-start(), calls=%async_computation.11 | async-start | bytes 4718592 | tf_op jit(solution)/shard_map/reduce_scatter | solution.py:248
  609.9 1191.2 %reduce-scatter.13.cloned.1.call-start = ((), (), s32[]{:S(2)}) async-start(), calls=%async_computation.12 | async-start | bytes 9437184 | tf_op jit(solution)/shard_map/reduce_scatter | solution.py:249
  616.7 93.4 %copy-start.5 = (bf16[512,2048]{1,0:T(8,128)(2,1)S(1)}, bf16[512,2048]{1,0:T(8,128)(2,1)}, u32[]{:S(2)}) copy-start(bf16[512,2048]{1,0:T(8,128)(2,1)} %param.19) | copy-start | bytes 6291460
  616.7 93.4 %copy-start.49 = (f32[2048]{0:T(1024)S(1)}, f32[2048]{0:T(1024)}, u32[]{:S(2)}) copy-start(f32[2048]{0:T(1024)} %param.22) | copy-start | bytes 24580
  616.7 93.4 %copy-start.52 = (f32[512]{0:T(512)S(1)}, f32[512]{0:T(512)}, u32[]{:S(2)}) copy-start(f32[512]{0:T(512)} %copy-done.51) | copy-start | bytes 6148
  616.7 93.4 %copy-start.54 = (f32[512]{0:T(512)S(1)}, f32[512]{0:T(512)}, u32[]{:S(2)}) copy-start(f32[512]{0:T(512)} %copy-done.53) | copy-start | bytes 6148
  754.9 5.7 copy-start.6
  754.9 6.0 copy-start.11
  754.9 7.5 copy-start.15
  762.4 1038.6 %copy-start.1 = (bf16[2048,512]{1,0:T(8,128)(2,1)S(1)}, bf16[2048,512]{1,0:T(8,128)(2,1)}, u32[]{:S(2)}) copy-start(bf16[2048,512]{1,0:T(8,128)(2,1)} %param.24) | copy-start | bytes 6291460
  (56 other events, 123.3 us)
Sparse Core Ops, SparseCore 0:
  20.3 127.2 all-gather.5
  182.1 83.6 all-reduce.10
  288.3 85.6 all-reduce.12
  407.9 124.5 all-gather.7
  559.0 151.0 all-reduce.14
  714.2 88.9 reduce-scatter.8
  807.3 147.0 reduce-scatter.18
  958.7 146.5 reduce-scatter.20
  1109.5 146.9 reduce-scatter.22
  1260.5 146.9 reduce-scatter.16
  1411.7 146.5 reduce-scatter.14
  1562.3 87.3 reduce-scatter.10
  1653.9 147.0 reduce-scatter.12
where the time goes:
time: 1810 us
  waiting for transfers between devices  1490 us (82%)
  matrix products  132 us (7%)
  other arithmetic  64.9 us (4%)
  blocking collectives  62.6 us (3%)
  local copies, waits for them, and re-layouts  41.1 us (2%)
    all_gather x2, waiting for transfers between devices, entering(): everything = jax.tree.map(lambda part: lax.all_gather(part, axis), x)  198 us
    reduce_scatter x1, waiting for transfers between devices, shards(): lax.psum_scatter(value_grad, 'seq', scatter_dimension=0, tiled=True)  151 us
    reduce_scatter x1, waiting for transfers between devices, shards(): lax.psum_scatter(up_grad, 'seq', scatter_dimension=0, tiled=True)  151 us
    reduce_scatter x1, waiting for transfers between devices, shards(): lax.psum_scatter(down_grad, 'seq', scatter_dimension=1, tiled=True)  151 us
    reduce_scatter x1, waiting for transfers between devices, shards(): lax.psum_scatter(output_grad, 'seq', scatter_dimension=1, tiled=True)  151 us
    reduce_scatter x1, waiting for transfers between devices, shards(): lax.psum_scatter(mlp_gate_grad, 'seq', scatter_dimension=0, tiled=True)  151 us
    reduce_scatter x1, waiting for transfers between devices, shards(): lax.psum_scatter(gate_grad, 'seq', scatter_dimension=0, tiled=True)  151 us
    psum x1, waiting for transfers between devices, shards(): lax.psum(jnp.dot(product, down_weight, preferred_element_type=jnp.float32...  92.6 us
  transfers between devices with their start and end apart: 13, of which 13 were waited for; matrix products, arithmetic and copies ran while one was open for 5% of the time, Pallas kernels for 0%

commit v1 on v0

v1 whole, which is shorter than its diff:
```python
import jax
import jax.numpy as jnp
from jax import lax
from jax.sharding import Mesh
from jax.sharding import PartitionSpec as P


KD = 256
VD = 512
SEQ = ("outer", "pair")

EPSILON = 1e-05
F32 = jnp.float32
BF16 = jnp.bfloat16
FULL_ACCURACY = lax.Precision.HIGHEST


def after(x, *events):
    return lax.optimization_barrier((x, *events))[0]


def widen(x):
    return lax.reduce_precision(x.astype(F32), 8, 7)


def narrow(x, zero):
    return (x + zero).astype(BF16)


def flip(x, axis, bit):
    count = lax.axis_size(axis)
    return lax.ppermute(x, axis, [(i, i ^ bit) for i in range(count)])


def bits_of(count):
    bits = []
    while (1 << len(bits)) < count:
        bits.append(1 << len(bits))
    assert (1 << len(bits)) == count
    return bits


def relative_order(count):
    order = [0]
    for bit in reversed(bits_of(count)):
        order = order + [j | bit for j in order]
    return order


def to_relative(x, axis_name, dim):
    count, own = lax.axis_size(axis_name), lax.axis_index(axis_name)
    size = x.shape[dim] // count
    return jnp.concatenate(
        [lax.dynamic_slice_in_dim(x, (own ^ j) * size, size, dim) for j in relative_order(count)],
        axis=dim,
    )


def from_relative(x, axis_name, dim):
    count, own = lax.axis_size(axis_name), lax.axis_index(axis_name)
    size = x.shape[dim] // count
    bits = bits_of(count)
    parts = []
    for i in range(count):
        j = own ^ i
        place = 0
        for n in range(len(bits)):
            place = place + ((j >> n) & 1) * (count >> (n + 1))
        parts.append(lax.dynamic_slice_in_dim(x, place * size, size, dim))
    return jnp.concatenate(parts, axis=dim)


def scatter_rows(x, axis_name):
    for bit in bits_of(lax.axis_size(axis_name)):
        half = x.shape[0] // 2
        x = x[:half] + flip(x[half:], axis_name, bit)
    return x


def gather_rows(x, axis_name):
    for bit in reversed(bits_of(lax.axis_size(axis_name))):
        x = jnp.concatenate([x, flip(x, axis_name, bit)], axis=0)
    return x


def layer_norm(values, scales, shifts):
    centred = values - jnp.mean(values, axis=-1, keepdims=True)
    inverse = lax.rsqrt(jnp.mean(centred * centred, axis=-1, keepdims=True) + EPSILON)
    normed = centred * inverse
    return (normed * scales + shifts, normed, inverse)


def norm_back(upstream, normed, inverse):
    return inverse * (
        upstream
        - jnp.mean(upstream, axis=-1, keepdims=True)
        - normed * jnp.mean(upstream * normed, axis=-1, keepdims=True)
    )


def gelu_pair(pre_act):
    normal_cdf = 0.5 * (1.0 + lax.erf(pre_act * 0.7071067811865476))
    density = jnp.exp(-0.5 * pre_act * pre_act) * 0.3989422804014327
    return (pre_act * normal_cdf, normal_cdf + pre_act * density)


def dot(a, b):
    return jnp.dot(a, b, preferred_element_type=F32)


def contract_rows(left_side, right_side, precision=None):
    return lax.dot_general(
        left_side,
        right_side,
        (((0,), (0,)), ((), ())),
        precision=precision,
        preferred_element_type=F32,
    )


def times_transpose(left_side, right_side, precision=None):
    return lax.dot_general(
        left_side,
        right_side,
        (((1,), (1,)), ((), ())),
        precision=precision,
        preferred_element_type=F32,
    )


def from_partner(x, zero):
    return narrow(flip(widen(x), "pair", 1), zero)


def carry_states(local, decay, suffix, event=None):
    pairs, odd = lax.axis_size("outer"), lax.axis_index("pair")
    if suffix:
        odd = 1 - odd
    half = local.shape[1] // 2
    keep = lax.dynamic_slice_in_dim(local, odd * half, half, 1)
    give = lax.dynamic_slice_in_dim(local, (1 - odd) * half, half, 1)
    got = flip(give, "pair", 1)
    if event is not None:
        got = after(got, event)
    earlier = jnp.where(odd == 0, keep, got)
    later = jnp.where(odd == 0, got, keep)
    step = decay[:, None, None]
    total = step * earlier + later

    def shifted(x, distance, first):
        moves = [(i, i + distance) for i in range(first, pairs - distance)]
        if suffix:
            moves = [(pairs - 1 - i, pairs - 1 - j) for i, j in moves]
        return lax.ppermute(x, "outer", moves)

    arriving = shifted(total, 1, 0)
    factor = step * step
    distance = 1
    while distance < pairs - 1:
        arriving = arriving + factor * shifted(arriving, distance, 1)
        factor = factor * factor
        distance *= 2
    second = step * arriving + earlier
    mine = jnp.where(odd == 0, arriving, second)
    other = jnp.where(odd == 0, second, arriving)
    rest = flip(other, "pair", 1)
    return jnp.where(
        odd == 0,
        jnp.concatenate([mine, rest], axis=1),
        jnp.concatenate([rest, mine], axis=1),
    )


def split_columns(x):
    outer, place = lax.axis_size("outer"), lax.axis_index("pair")
    size = x.shape[1] // (2 * outer)

    def blocks(which):
        return jnp.concatenate(
            [lax.dynamic_slice_in_dim(x, (2 * o + which) * size, size, 1) for o in range(outer)],
            axis=1,
        )

    return blocks(place), blocks(1 - place)


def sum_blocks(x, dim):
    return lax.psum_scatter(x, "outer", scatter_dimension=dim, tiled=True)


def shards(
    block_input,
    out_cotangent,
    decay_rate,
    first_scale,
    first_shift,
    query_weight,
    key_weight,
    value_weight,
    gate_weight,
    output_weight,
    second_scale,
    second_shift,
    up_weight,
    mlp_gate_weight,
    down_weight,
):
    length, _ = block_input.shape
    local_heads = decay_rate.shape[0]
    head_range = range(local_heads)
    zero = decay_rate[0] * 0.0

    places = jnp.arange(length, dtype=F32)
    distance = places[:, None] - places[None, :]
    causal = distance >= 0.0
    safe = jnp.where(causal, distance, 0.0)
    masks = [jnp.where(causal, jnp.exp(-decay_rate[h] * safe), 0.0) for h in head_range]
    fade_in = [jnp.exp(-places * decay_rate[h])[:, None] for h in head_range]
    fade_out = [jnp.exp(-(length - places) * decay_rate[h])[:, None] for h in head_range]
    block_decay = jnp.exp(-decay_rate * length)

    inputs = block_input.astype(F32)
    first_out, first_normed, first_inverse = layer_norm(inputs, first_scale, first_shift)
    first_act = first_out.astype(BF16)
    queries = dot(first_act, query_weight).astype(BF16)
    key_rows = dot(first_act, key_weight).astype(BF16)
    value_rows = dot(first_act, value_weight).astype(BF16)
    q = [queries[:, h * KD : (h + 1) * KD] for h in head_range]
    k = [key_rows[:, h * KD : (h + 1) * KD] for h in head_range]
    v = [value_rows[:, h * VD : (h + 1) * VD] for h in head_range]
    local_state = jnp.stack(
        [
            contract_rows(k[h].astype(F32) * fade_out[h], v[h].astype(F32), FULL_ACCURACY)
            for h in head_range
        ]
    )
    state_in = carry_states(local_state, block_decay, False)

    gate_pre = dot(first_act, gate_weight)
    sigmoid_gate = jax.nn.sigmoid(gate_pre)
    swish_gate = gate_pre * sigmoid_gate
    retain_weights = [(times_transpose(q[h], k[h]) * masks[h]).astype(BF16) for h in head_range]
    group_normed, spread = [], []
    for h in head_range:
        retained = dot(retain_weights[h], v[h]) + fade_in[h] * jnp.dot(
            q[h].astype(F32), state_in[h], precision=FULL_ACCURACY
        )
        centred = retained - jnp.mean(retained, axis=-1, keepdims=True)
        inverse = lax.rsqrt(jnp.mean(centred * centred, axis=-1, keepdims=True) + EPSILON)
        group_normed.append(centred * inverse)
        spread.append(inverse)
    gated_rows = jnp.concatenate(
        [swish_gate[:, h * VD : (h + 1) * VD] * group_normed[h] for h in head_range], axis=1
    ).astype(BF16)
    gated_rel = to_relative(gated_rows, "head", 0)
    own_rows = length // lax.axis_size("head")
    row_start = lax.axis_index("head") * own_rows
    input_rows = lax.dynamic_slice_in_dim(inputs, row_start, own_rows, 0)
    cot_rows = lax.dynamic_slice_in_dim(out_cotangent, row_start, own_rows, 0).astype(F32)

    cot_rel = to_relative(out_cotangent, "head", 0)
    cot_kept, cot_given = split_columns(cot_rel)
    cot_pair = jnp.concatenate([cot_kept, from_partner(after(cot_given, state_in), zero)])

    hidden = input_rows + scatter_rows(dot(gated_rel, output_weight), "head")
    second_out, second_normed, second_inverse = layer_norm(hidden, second_scale, second_shift)
    second_rows = widen(second_out)
    second_act = narrow(gather_rows(second_rows, "head"), zero)
    second_given = flip(split_columns(second_rows)[1], "pair", 1)

    first_kept, first_given = split_columns(first_act)
    first_given = flip(after(widen(first_given), second_rows), "pair", 1)

    up_pre = dot(second_act, up_weight)
    mlp_pre = dot(second_act, mlp_gate_weight)
    gelu_value, gelu_slope = gelu_pair(mlp_pre)
    product = (gelu_value * up_pre).astype(BF16)
    product_given = flip(widen(product), "pair", 1)

    product_grad = times_transpose(cot_rel, down_weight)
    up_pre_grad = (product_grad * gelu_value).astype(BF16)
    mlp_pre_grad = (product_grad * up_pre * gelu_slope).astype(BF16)
    mlp_grads = jnp.concatenate([up_pre_grad, mlp_pre_grad], axis=1)
    mlp_given = flip(widen(mlp_grads), "pair", 1)
    second_act_grad = scatter_rows(
        times_transpose(up_pre_grad, up_weight) + times_transpose(mlp_pre_grad, mlp_gate_weight),
        "head",
    )
    hidden_grad = cot_rows + norm_back(
        second_act_grad * second_scale, second_normed, second_inverse
    )
    cast_rows = widen(hidden_grad)
    cast_all = gather_rows(cast_rows, "head")

    product_pair = jnp.concatenate([product, narrow(after(product_given, cast_rows), zero)])
    down_term = contract_rows(cot_pair, product_pair)
    down_grad = sum_blocks(down_term, 0).T

    hidden_cast = from_relative(narrow(after(cast_all, down_term), zero), "head", 0)
    gated_grad = times_transpose(hidden_cast, output_weight)
    group_flat = jnp.concatenate(group_normed, axis=1)
    gate_pre_grad = (
        gated_grad * group_flat * sigmoid_gate * (1.0 + gate_pre * (1.0 - sigmoid_gate))
    ).astype(BF16)
    normed_grad = gated_grad * swish_gate
    retained_grad = [
        norm_back(normed_grad[:, h * VD : (h + 1) * VD], group_normed[h], spread[h]).astype(BF16)
        for h in head_range
    ]
    state_term = jnp.stack(
        [
            contract_rows(
                q[h].astype(F32) * fade_in[h], retained_grad[h].astype(F32), FULL_ACCURACY
            )
            for h in head_range
        ]
    )
    cast_given = flip(split_columns(cast_rows)[1], "pair", 1)
    gated_given = flip(after(widen(gated_rows), cast_rows), "pair", 1)
    gate_given = flip(widen(gate_pre_grad), "pair", 1)

    second_given = narrow(gather_rows(second_given, "head"), zero)
    second_pair = jnp.concatenate([split_columns(second_act)[0], second_given])
    mlp_pair = jnp.concatenate([mlp_grads, narrow(after(mlp_given, state_term), zero)])
    mlp_term = contract_rows(second_pair, mlp_pair)
    up_both = sum_blocks(mlp_term, 0)
    state_grad = carry_states(state_term, block_decay, True, mlp_term)
    hidden_units = up_weight.shape[1]
    up_grad, mlp_gate_grad = up_both[:, :hidden_units], up_both[:, hidden_units:]

    output_rows = hidden + scatter_rows(dot(product, after(down_weight, cast_rows)), "head")
    output_rows = widen(output_rows)
    block_output = from_relative(narrow(gather_rows(output_rows, "head"), zero), "head", 0)

    second_scale_part = jnp.sum(second_act_grad * second_normed, axis=0)
    second_shift_part = jnp.sum(second_act_grad, axis=0)

    query_parts, key_parts, value_parts = [], [], []
    for h in head_range:
        score_grad = (times_transpose(retained_grad[h], v[h]) * masks[h]).astype(BF16)
        query_parts.append(
            dot(score_grad, k[h])
            + fade_in[h]
            * times_transpose(retained_grad[h].astype(F32), state_in[h], FULL_ACCURACY)
        )
        key_parts.append(
            contract_rows(score_grad, q[h])
            + fade_out[h] * times_transpose(v[h].astype(F32), state_grad[h], FULL_ACCURACY)
        )
        value_parts.append(
            contract_rows(retain_weights[h], retained_grad[h])
            + fade_out[h]
            * jnp.dot(k[h].astype(F32), state_grad[h], precision=FULL_ACCURACY)
        )
    head_grads = jnp.concatenate(query_parts + key_parts + value_parts, axis=1).astype(BF16)
    head_given = flip(widen(head_grads), "pair", 1)

    cast_given = from_relative(narrow(gather_rows(cast_given, "head"), zero), "head", 0)
    cast_pair = jnp.concatenate([split_columns(hidden_cast)[0], cast_given])
    gated_pair = jnp.concatenate([gated_rows, narrow(gated_given, zero)])
    first_pair = jnp.concatenate([first_kept, narrow(after(first_given, head_grads), zero)])
    gate_pair = jnp.concatenate([gate_pre_grad, narrow(gate_given, zero)])
    output_term = jnp.concatenate(
        [contract_rows(cast_pair, gated_pair), contract_rows(first_pair, gate_pair)], axis=1
    )
    output_both = sum_blocks(output_term, 0)
    output_columns = gated_rows.shape[1]
    output_grad, gate_grad = output_both[:, :output_columns].T, output_both[:, output_columns:]

    head_pair = jnp.concatenate([head_grads, narrow(after(head_given, output_term), zero)])
    head_both = sum_blocks(contract_rows(first_pair, head_pair), 0)
    key_columns, value_columns = local_heads * KD, 2 * local_heads * KD
    query_grad = head_both[:, :key_columns]
    key_grad = head_both[:, key_columns:value_columns]
    value_grad = head_both[:, value_columns:]

    first_act_grad = (
        times_transpose(head_grads[:, :key_columns], query_weight)
        + times_transpose(head_grads[:, key_columns:value_columns], key_weight)
        + times_transpose(head_grads[:, value_columns:], value_weight)
        + times_transpose(gate_pre_grad, gate_weight)
    )
    first_act_grad = scatter_rows(to_relative(first_act_grad, "head", 0), "head")
    normed_rows = lax.dynamic_slice_in_dim(first_normed, row_start, own_rows, 0)
    inverse_rows = lax.dynamic_slice_in_dim(first_inverse, row_start, own_rows, 0)
    first_scale_part = jnp.sum(first_act_grad * normed_rows, axis=0)
    first_shift_part = jnp.sum(first_act_grad, axis=0)
    grad_rows = hidden_grad + norm_back(first_act_grad * first_scale, normed_rows, inverse_rows)
    grad_rows = widen(grad_rows)
    input_grad = from_relative(narrow(gather_rows(grad_rows, "head"), zero), "head", 0)

    vectors = jnp.stack([first_scale_part, first_shift_part, second_scale_part, second_shift_part])
    kept, given = split_columns(vectors)
    vectors = kept + flip(given, "pair", 1)
    vectors = to_relative(vectors, "outer", 1)
    for bit in bits_of(lax.axis_size("outer")):
        half = vectors.shape[1] // 2
        vectors = vectors[:, :half] + flip(vectors[:, half:], "outer", bit)
    for bit in bits_of(lax.axis_size("head")):
        vectors = vectors + flip(vectors, "head", bit)
    return (
        block_output,
        input_grad,
        vectors[0],
        vectors[1],
        query_grad,
        key_grad,
        value_grad,
        gate_grad,
        output_grad,
        vectors[2],
        vectors[3],
        up_grad,
        mlp_gate_grad,
        down_grad,
    )


def solution(mesh):
    seq, head = mesh.shape["seq"], mesh.shape["head"]
    mesh = Mesh(mesh.devices.reshape(seq // 2, 2, head), ("outer", "pair", "head"))
    in_specs = (
        P(SEQ, None),
        P(SEQ, None),
        P("head"),
        P(),
        P(),
        P(None, "head"),
        P(None, "head"),
        P(None, "head"),
        P(None, "head"),
        P("head", None),
        P(),
        P(),
        P(None, "head"),
        P(None, "head"),
        P("head", None),
    )
    out_specs = (
        P(SEQ, None),
        P(SEQ, None),
        P(SEQ),
        P(SEQ),
        P(SEQ, "head"),
        P(SEQ, "head"),
        P(SEQ, "head"),
        P(SEQ, "head"),
        P("head", SEQ),
        P(SEQ),
        P(SEQ),
        P(SEQ, "head"),
        P(SEQ, "head"),
        P("head", SEQ),
    )

    def step(*args):
        return shards(*args)

    step = jax.shard_map(step, mesh=mesh, in_specs=in_specs, out_specs=out_specs, check_vma=False)
    return step
```

time: 1810 us -> 942 us (0.52)
  waiting for transfers between devices: 1490 us -> 653 us
  blocking collectives: 62.6 us -> 0 us
  starting transfers between devices: 1.97 us -> 53.9 us
  matrix products: 132 us -> 105 us
    reduce_scatter x8 -> x4, waiting for transfers between devices: 1040 us -> 49.3 us  [sum_blocks(): return lax.psum_scatter(x, 'outer', scatter_dimension=dim, tiled=True)]
    ppermute x0 -> x44, waiting for transfers between devices: none -> 604 us  [the longest x38 531 us: flip(): return lax.ppermute(x, axis, [(i, i ^ bit) for i in range(count)])]
    psum x3 -> x0, waiting for transfers between devices: 255 us -> none  [the longest x1 92.6 us: shards(): lax.psum(jnp.dot(product, down_weight, preferred_element_type=jnp.float32...]
    all_gather x2 -> x0, waiting for transfers between devices: 198 us -> none  [entering(): everything = jax.tree.map(lambda part: lax.all_gather(part, axis), x)]
    unnamed x2 -> x0, blocking collectives: 62.6 us -> none
    ppermute x0 -> x44, starting transfers between devices: none -> 53.2 us  [the longest x38 42 us: flip(): return lax.ppermute(x, axis, [(i, i ^ bit) for i in range(count)])]
    dot_general x36 -> x45, matrix products: 132 us -> 105 us  [the longest x12 40.7 us: dot(): return jnp.dot(a, b, preferred_element_type=F32)]
    select_n x17 -> x4, other arithmetic: 26.1 us -> 0.74 us  [the longest x2 0.52 us: carry_states(): mine = jnp.where(odd == 0, arriving, second)]
  transfers between devices with their start and end apart: 13 -> 48, of which waited for: 13 -> 31; matrix products, arithmetic and copies ran while one was open for 5% -> 14% of each run, Pallas kernels for 0% -> 0%
where the time goes in v1:
time: 942 us; the launch traced here: 934 us
  waiting for transfers between devices  653 us (69%)
  matrix products  105 us (11%)
  other arithmetic  64.9 us (7%)
  starting transfers between devices  53.9 us (6%)
  local copies, waits for them, and re-layouts  39.5 us (4%)
  between operations  18.1 us (2%)
    ppermute x38, waiting for transfers between devices, flip(): return lax.ppermute(x, axis, [(i, i ^ bit) for i in range(count)])  531 us
    ppermute x6, waiting for transfers between devices, shifted(): return lax.ppermute(x, 'outer', moves)  72.9 us
    reduce_scatter x4, waiting for transfers between devices, sum_blocks(): return lax.psum_scatter(x, 'outer', scatter_dimension=dim, tiled=True)  49.3 us
    ppermute x38, starting transfers between devices, flip(): return lax.ppermute(x, axis, [(i, i ^ bit) for i in range(count)])  42 us
    dot_general x12, matrix products, dot(): return jnp.dot(a, b, preferred_element_type=F32)  40.7 us
    dot_general x13, matrix products, contract_rows(): lax.dot_general(left_side, right_side, (((0,), (0,)), ((), ())), precisio...  31.2 us
    dot_general x16, matrix products, times_transpose(): lax.dot_general(left_side, right_side, (((1,), (1,)), ((), ())), precisio...  28.4 us
    unnamed x201, local copies, waits for them, and re-layouts  19.6 us
  transfers between devices with their start and end apart: 48, of which 31 were waited for; matrix products, arithmetic and copies ran while one was open for 14% of the time, Pallas kernels for 0%

profile of v1, /device:TPU:0, one launch (start us, length us, event | category | flops | bytes accessed | tf_op | source)
XLA Modules:
  0.0 934.1 jit_solution(16923719792218976993)
XLA Ops:
  26.9 12.2 %collective-permute-done = f32[2,128,512]{2,1,0:T(8,128)} collective-permute-done((f32[2,128,512]{2,1,0:T(8,128)}, f32[2,128,512]{2,1,0:T(8,128)}, u32[]{:S(2)}, u32[]{:S(2)}) %collective-permute-start) | collective-permute-done | bytes 524320 | tf_op jit(solution)/shard_map/ppermute | solution.py:32
  41.2 4.6 collective-permute-start.1
  45.8 6.7 fusion.56
  69.8 9.2 collective-permute-done.4
  94.2 23.1 %collective-permute-done.6 = f32[128,2048]{1,0:T(8,128)S(1)} collective-permute-done((f32[128,2048]{1,0:T(8,128)S(1)}, f32[128,2048]{1,0:T(8,128)S(1)}, u32[]{:S(2)}, u32[]{:S(2)}) %collective-permute-start.6) | collective-permute-done | bytes 1048608 | tf_op jit(solution)/shard_map/ppermute | solution.py:32
  119.7 22.8 %collective-permute-done.7 = f32[128,2048]{1,0:T(8,128)S(1)} collective-permute-done((f32[128,2048]{1,0:T(8,128)S(1)}, f32[128,2048]{1,0:T(8,128)S(1)}, u32[]{:S(2)}, u32[]{:S(2)}) %collective-permute-start.7) | collective-permute-done | bytes 1048608 | tf_op jit(solution)/shard_map/ppermute | solution.py:32
  153.0 14.2 %fusion.180 = f32[512,1024]{1,0:T(8,128)S(1)} fusion(bf16[512,2048]{1,0:T(8,128)(2,1)S(1)} %fusion, bf16[2048,1024]{1,0:T(8,128)(2,1)S(1)} %copy-done.87), kind=kOutput, calls=%fused_computation.418 | convolution fusion | flops 2147483648 | bytes 8388608 | tf_op jit(solution)/shard_map/dot_general | solution.py:108
  167.2 4.6 convert_reduce-precision_fusion.5
  189.3 41.5 %collective-permute-done.17 = f32[512,1024]{1,0:T(8,128)S(1)} collective-permute-done((f32[512,1024]{1,0:T(8,128)S(1)}, f32[512,1024]{1,0:T(8,128)S(1)}, u32[]{:S(2)}, u32[]{:S(2)}) %collective-permute-start.17) | collective-permute-done | bytes 2097184 | tf_op jit(solution)/shard_map/ppermute | solution.py:32
  234.0 40.8 %collective-permute-done.18 = f32[512,1024]{1,0:T(8,128)S(1)} collective-permute-done((f32[512,1024]{1,0:T(8,128)S(1)}, f32[512,1024]{1,0:T(8,128)S(1)}, u32[]{:S(2)}, u32[]{:S(2)}) %collective-permute-start.18) | collective-permute-done | bytes 2097184 | tf_op jit(solution)/shard_map/ppermute | solution.py:32
  275.0 4.3 fusion.19
  283.9 100.7 %collective-permute-done.20 = f32[128,1024]{1,0:T(8,128)S(1)} collective-permute-done((f32[128,1024]{1,0:T(8,128)S(1)}, f32[128,1024]{1,0:T(8,128)S(1)}, u32[]{:S(2)}, u32[]{:S(2)}) %collective-permute-start.20) | collective-permute-done | bytes 524320 | tf_op jit(solution)/shard_map/ppermute | solution.py:32
  386.1 10.6 %collective-permute-done.21 = f32[128,1024]{1,0:T(8,128)S(1)} collective-permute-done((f32[128,1024]{1,0:T(8,128)S(1)}, f32[128,1024]{1,0:T(8,128)S(1)}, u32[]{:S(2)}, u32[]{:S(2)}) %collective-permute-start.21) | collective-permute-done | bytes 524320 | tf_op jit(solution)/shard_map/ppermute | solution.py:32
  401.5 8.0 fusion.2
  416.4 11.1 %collective-permute-done.39 = f32[128,1024]{1,0:T(8,128)S(1)} collective-permute-done((f32[128,1024]{1,0:T(8,128)S(1)}, f32[128,1024]{1,0:T(8,128)S(1)}, u32[]{:S(2)}, u32[]{:S(2)}) %collective-permute-start.39) | collective-permute-done | bytes 524320 | tf_op jit(solution)/shard_map/ppermute | solution.py:32
  428.1 8.1 collective-permute-done.15
  437.9 8.7 collective-permute-done.40
  453.1 19.5 %collective-permute-done.42 = f32[512,1024]{1,0:T(8,128)} collective-permute-done((f32[512,1024]{1,0:T(8,128)}, f32[512,1024]{1,0:T(8,128)}, u32[]{:S(2)}, u32[]{:S(2)}) %collective-permute-start.42) | collective-permute-done | bytes 2097184 | tf_op jit(solution)/shard_map/ppermute | solution.py:32
  479.4 6.6 convert_reduce-precision_fusion.2
  496.0 32.7 %collective-permute-done.19 = f32[2,128,512]{2,1,0:T(8,128)S(1)} collective-permute-done((f32[2,128,512]{2,1,0:T(8,128)S(1)}, f32[2,128,512]{2,1,0:T(8,128)S(1)}, u32[]{:S(2)}, u32[]{:S(2)}) %collective-permute-start.19) | collective-permute-done | bytes 524320 | tf_op jit(solution)/shard_map/ppermute | solution.py:32
  531.7 49.1 %collective-permute-done.24 = f32[2,128,512]{2,1,0:T(8,128)S(1)} collective-permute-done((f32[2,128,512]{2,1,0:T(8,128)S(1)}, f32[2,128,512]{2,1,0:T(8,128)S(1)}, u32[]{:S(2)}, u32[]{:S(2)}) %collective-permute-start.24) | collective-permute-done | bytes 524320 | tf_op jit(solution)/shard_map/ppermute | solution.py:154
  584.0 11.8 %collective-permute-done.25 = f32[2,128,512]{2,1,0:T(8,128)S(1)} collective-permute-done((f32[2,128,512]{2,1,0:T(8,128)S(1)}, f32[2,128,512]{2,1,0:T(8,128)S(1)}, u32[]{:S(2)}, u32[]{:S(2)}) %collective-permute-start.25) | collective-permute-done | bytes 524320 | tf_op jit(solution)/shard_map/ppermute | solution.py:154
  599.7 9.3 collective-permute-done.26
  611.2 7.5 collective-permute-done.27
  636.0 86.0 %collective-permute-done.38 = f32[512,2048]{1,0:T(8,128)S(1)} collective-permute-done((f32[512,2048]{1,0:T(8,128)S(1)}, f32[512,2048]{1,0:T(8,128)S(1)}, u32[]{:S(2)}, u32[]{:S(2)}) %collective-permute-start.38) | collective-permute-done | bytes 4194336 | tf_op jit(solution)/shard_map/ppermute | solution.py:32
  722.5 8.0 fusion.9
  730.5 4.8 fusion.182
  754.7 19.1 %collective-permute-done.12 = f32[128,2048]{1,0:T(8,128)S(1)} collective-permute-done((f32[128,2048]{1,0:T(8,128)S(1)}, f32[128,2048]{1,0:T(8,128)S(1)}, u32[]{:S(2)}, u32[]{:S(2)}) %collective-permute-start.12) | collective-permute-done | bytes 1048608 | tf_op jit(solution)/shard_map/ppermute | solution.py:32
  776.1 20.1 %collective-permute-done.29 = f32[128,2048]{1,0:T(8,128)S(1)} collective-permute-done((f32[128,2048]{1,0:T(8,128)S(1)}, f32[128,2048]{1,0:T(8,128)S(1)}, u32[]{:S(2)}, u32[]{:S(2)}) %collective-permute-start.29) | collective-permute-done | bytes 1048608 | tf_op jit(solution)/shard_map/ppermute | solution.py:32
  800.0 18.8 %collective-permute-done.13 = f32[128,2048]{1,0:T(8,128)S(1)} collective-permute-done((f32[128,2048]{1,0:T(8,128)S(1)}, f32[128,2048]{1,0:T(8,128)S(1)}, u32[]{:S(2)}, u32[]{:S(2)}) %collective-permute-start.13) | collective-permute-done | bytes 1048608 | tf_op jit(solution)/shard_map/ppermute | solution.py:32
  820.4 20.6 %collective-permute-done.30 = f32[128,2048]{1,0:T(8,128)S(1)} collective-permute-done((f32[128,2048]{1,0:T(8,128)S(1)}, f32[128,2048]{1,0:T(8,128)S(1)}, u32[]{:S(2)}, u32[]{:S(2)}) %collective-permute-start.30) | collective-permute-done | bytes 1048608 | tf_op jit(solution)/shard_map/ppermute | solution.py:32
  874.3 49.3 %reduce-scatter.5.cloned.1.call-done = f32[256,2048]{1,0:T(8,128)} async-done(((f32[1024,2048]{1,0:T(8,128)}), f32[256,2048]{1,0:T(8,128)}) %reduce-scatter.5.cloned.1.call-update) | async-done | bytes 2097168 | tf_op jit(solution)/shard_map/reduce_scatter | solution.py:188
  (438 shorter events, 221.3 us)
Async XLA Ops:
  7.2 852.8 %reduce-scatter.11.cloned.1.call-start = ((), (), s32[]{:S(2)}) async-start(), calls=%async_computation.7 | async-start | bytes 5242880 | tf_op jit(solution)/shard_map/reduce_scatter | solution.py:188
  24.0 15.2 %collective-permute-start = (f32[2,128,512]{2,1,0:T(8,128)}, f32[2,128,512]{2,1,0:T(8,128)}, u32[]{:S(2)}, u32[]{:S(2)}) collective-permute-start(f32[2,128,512]{2,1,0:T(8,128)} %fusion.94), channel_id=1, source_target_pairs={{0,4},{4,0},{1,5},{5,1},{2,6},{6,2},{3,7},{7,3},{8,12},{12,8},{9,1... | collective-permute-start | bytes 1572872 | tf_op jit(solution)/shard_map/ppermute | solution.py:32
  41.2 14.0 %collective-permute-start.1 = (f32[2,128,512]{2,1,0:T(8,128)S(1)}, f32[2,128,512]{2,1,0:T(8,128)}, u32[]{:S(2)}, u32[]{:S(2)}) collective-permute-start(f32[2,128,512]{2,1,0:T(8,128)S(1)} %get-tuple-element.76), channel_id=1, source_target_pairs={{0,8},{8,16},{16,24},{1,9},{9,17},{17,25},{2,10},{10,18},{18,26},{... | collective-permute-start | bytes 1572872 | tf_op jit(solution)/shard_map/ppermute | solution.py:154
  66.2 12.8 %collective-permute-start.4 = (f32[2,128,512]{2,1,0:T(8,128)S(1)}, f32[2,128,512]{2,1,0:T(8,128)S(1)}, u32[]{:S(2)}, u32[]{:S(2)}) collective-permute-start(f32[2,128,512]{2,1,0:T(8,128)S(1)} %get-tuple-element.89), channel_id=1, source_target_pairs={{0,4},{4,0},{1,5},{5,1},{2,6},{6,2},{3,7},{7,3},{8,12},{12,8},{9,1... | collective-permute-start | bytes 1572872 | tf_op jit(solution)/shard_map/ppermute | solution.py:32
  92.1 25.3 %collective-permute-start.6 = (f32[128,2048]{1,0:T(8,128)S(1)}, f32[128,2048]{1,0:T(8,128)S(1)}, u32[]{:S(2)}, u32[]{:S(2)}) collective-permute-start(f32[128,2048]{1,0:T(8,128)S(1)} %slice.208), channel_id=1, source_target_pairs={{0,2},{1,3},{2,0},{3,1},{4,6},{5,7},{6,4},{7,5},{8,10},{9,11},{10,... | collective-permute-start | bytes 3145736 | tf_op jit(solution)/shard_map/ppermute | solution.py:32
  118.2 24.4 %collective-permute-start.7 = (f32[128,2048]{1,0:T(8,128)S(1)}, f32[128,2048]{1,0:T(8,128)S(1)}, u32[]{:S(2)}, u32[]{:S(2)}) collective-permute-start(f32[128,2048]{1,0:T(8,128)S(1)} %add_reduce-precision_fusion.1), channel_id=1, source_target_pairs={{0,2},{1,3},{2,0},{3,1},{4,6},{5,7},{6,4},{7,5},{8,10},{9,11},{10,... | collective-permute-start | bytes 3145736 | tf_op jit(solution)/shard_map/ppermute | solution.py:32
  182.2 48.6 %collective-permute-start.17 = (f32[512,1024]{1,0:T(8,128)S(1)}, f32[512,1024]{1,0:T(8,128)S(1)}, u32[]{:S(2)}, u32[]{:S(2)}) collective-permute-start(f32[512,1024]{1,0:T(8,128)S(1)} %convert_reduce-precision_fusion.6), channel_id=1, source_target_pairs={{0,4},{4,0},{1,5},{5,1},{2,6},{6,2},{3,7},{7,3},{8,12},{12,8},{9,1... | collective-permute-start | bytes 6291464 | tf_op jit(solution)/shard_map/ppermute | solution.py:32
  186.0 45.1 %collective-permute-start.10 = (f32[128,2048]{1,0:T(8,128)S(1)}, f32[128,2048]{1,0:T(8,128)S(1)}, u32[]{:S(2)}, u32[]{:S(2)}) collective-permute-start(f32[128,2048]{1,0:T(8,128)S(1)} %slice.212), channel_id=1, source_target_pairs={{0,2},{1,3},{2,0},{3,1},{4,6},{5,7},{6,4},{7,5},{8,10},{9,11},{10,... | collective-permute-start | bytes 3145736 | tf_op jit(solution)/shard_map/ppermute | solution.py:32
  187.6 87.2 %collective-permute-start.18 = (f32[512,1024]{1,0:T(8,128)S(1)}, f32[512,1024]{1,0:T(8,128)S(1)}, u32[]{:S(2)}, u32[]{:S(2)}) collective-permute-start(f32[512,1024]{1,0:T(8,128)S(1)} %copy-done.94), channel_id=1, source_target_pairs={{0,4},{4,0},{1,5},{5,1},{2,6},{6,2},{3,7},{7,3},{8,12},{12,8},{9,1... | collective-permute-start | bytes 6291464 | tf_op jit(solution)/shard_map/ppermute | solution.py:32
  279.4 587.8 %reduce-scatter.9.cloned.1.call-start = ((), (), s32[]{:S(2)}) async-start(), calls=%async_computation.6 | async-start | bytes 10485760 | tf_op jit(solution)/shard_map/reduce_scatter | solution.py:188
  281.6 118.3 %collective-permute-start.23 = (f32[512,2048]{1,0:T(8,128)S(1)}, f32[512,2048]{1,0:T(8,128)S(1)}, u32[]{:S(2)}, u32[]{:S(2)}) collective-permute-start(f32[512,2048]{1,0:T(8,128)S(1)} %convert_reduce-precision_fusion.1), channel_id=1, source_target_pairs={{0,4},{4,0},{1,5},{5,1},{2,6},{6,2},{3,7},{7,3},{8,12},{12,8},{9,1... | collective-permute-start | bytes 12582920 | tf_op jit(solution)/shard_map/ppermute | solution.py:32
  283.5 101.0 %collective-permute-start.20 = (f32[128,1024]{1,0:T(8,128)S(1)}, f32[128,1024]{1,0:T(8,128)S(1)}, u32[]{:S(2)}, u32[]{:S(2)}) collective-permute-start(f32[128,1024]{1,0:T(8,128)S(1)} %pad_maximum_fusion.17), channel_id=1, source_target_pairs={{0,4},{4,0},{1,5},{5,1},{2,6},{6,2},{3,7},{7,3},{8,12},{12,8},{9,1... | collective-permute-start | bytes 1572872 | tf_op jit(solution)/shard_map/ppermute | solution.py:32
  409.5 460.9 %reduce-scatter.7.cloned.1.call-start = ((), (), s32[]{:S(2)}) async-start(), calls=%async_computation.5 | async-start | bytes 10485760 | tf_op jit(solution)/shard_map/reduce_scatter | solution.py:188
  410.0 26.3 %collective-permute-start.15 = (f32[128,2048]{1,0:T(8,128)}, f32[128,2048]{1,0:T(8,128)S(1)}, u32[]{:S(2)}, u32[]{:S(2)}) collective-permute-start(f32[128,2048]{1,0:T(8,128)} %get-tuple-element.67), channel_id=1, source_target_pairs={{0,2},{1,3},{2,0},{3,1},{4,6},{5,7},{6,4},{7,5},{8,10},{9,11},{10,... | collective-permute-start | bytes 3145736 | tf_op jit(solution)/shard_map/ppermute | solution.py:32
  412.7 14.9 %collective-permute-start.39 = (f32[128,1024]{1,0:T(8,128)S(1)}, f32[128,1024]{1,0:T(8,128)S(1)}, u32[]{:S(2)}, u32[]{:S(2)}) collective-permute-start(f32[128,1024]{1,0:T(8,128)S(1)} %pad_maximum_fusion.18), channel_id=1, source_target_pairs={{0,4},{4,0},{1,5},{5,1},{2,6},{6,2},{3,7},{7,3},{8,12},{12,8},{9,1... | collective-permute-start | bytes 1572872 | tf_op jit(solution)/shard_map/ppermute | solution.py:32
  416.2 56.5 %collective-permute-start.42 = (f32[512,1024]{1,0:T(8,128)}, f32[512,1024]{1,0:T(8,128)}, u32[]{:S(2)}, u32[]{:S(2)}) collective-permute-start(f32[512,1024]{1,0:T(8,128)} %convert_reduce-precision_fusion.3), channel_id=1, source_target_pairs={{0,4},{4,0},{1,5},{5,1},{2,6},{6,2},{3,7},{7,3},{8,12},{12,8},{9,1... | collective-permute-start | bytes 6291464 | tf_op jit(solution)/shard_map/ppermute | solution.py:32
  427.6 19.1 %collective-permute-start.40 = (f32[128,1024]{1,0:T(8,128)S(1)}, f32[128,1024]{1,0:T(8,128)S(1)}, u32[]{:S(2)}, u32[]{:S(2)}) collective-permute-start(f32[128,1024]{1,0:T(8,128)S(1)} %collective-permute-done.39), channel_id=1, source_target_pairs={{0,2},{1,3},{2,0},{3,1},{4,6},{5,7},{6,4},{7,5},{8,10},{9,11},{10,... | collective-permute-start | bytes 1572872 | tf_op jit(solution)/shard_map/ppermute | solution.py:32
  437.9 36.6 %collective-permute-start.16 = (f32[256,2048]{1,0:T(8,128)}, f32[256,2048]{1,0:T(8,128)}, u32[]{:S(2)}, u32[]{:S(2)}) collective-permute-start(f32[256,2048]{1,0:T(8,128)} %pad_maximum_fusion.6), channel_id=1, source_target_pairs={{0,1},{1,0},{2,3},{3,2},{4,5},{5,4},{6,7},{7,6},{8,9},{9,8},{10,11... | collective-permute-start | bytes 6291464 | tf_op jit(solution)/shard_map/ppermute | solution.py:32
  449.8 173.9 %collective-permute-start.37 = (f32[512,1024]{1,0:T(8,128)S(1)}, f32[512,1024]{1,0:T(8,128)S(1)}, u32[]{:S(2)}, u32[]{:S(2)}) collective-permute-start(f32[512,1024]{1,0:T(8,128)S(1)} %convert_reduce-precision_fusion.4), channel_id=1, source_target_pairs={{0,4},{4,0},{1,5},{5,1},{2,6},{6,2},{3,7},{7,3},{8,12},{12,8},{9,1... | collective-permute-start | bytes 6291464 | tf_op jit(solution)/shard_map/ppermute | solution.py:32
  488.9 39.8 %collective-permute-start.19 = (f32[2,128,512]{2,1,0:T(8,128)S(1)}, f32[2,128,512]{2,1,0:T(8,128)S(1)}, u32[]{:S(2)}, u32[]{:S(2)}) collective-permute-start(f32[2,128,512]{2,1,0:T(8,128)S(1)} %fusion.97), channel_id=1, source_target_pairs={{0,4},{4,0},{1,5},{5,1},{2,6},{6,2},{3,7},{7,3},{8,12},{12,8},{9,1... | collective-permute-start | bytes 1572872 | tf_op jit(solution)/shard_map/ppermute | solution.py:32
  490.7 120.2 %collective-permute-start.43 = (f32[512,1024]{1,0:T(8,128)S(1)}, f32[512,1024]{1,0:T(8,128)S(1)}, u32[]{:S(2)}, u32[]{:S(2)}) collective-permute-start(f32[512,1024]{1,0:T(8,128)S(1)} %get-tuple-element.60), channel_id=1, source_target_pairs={{0,4},{4,0},{1,5},{5,1},{2,6},{6,2},{3,7},{7,3},{8,12},{12,8},{9,1... | collective-permute-start | bytes 6291464 | tf_op jit(solution)/shard_map/ppermute | solution.py:32
  528.9 51.9 %collective-permute-start.24 = (f32[2,128,512]{2,1,0:T(8,128)S(1)}, f32[2,128,512]{2,1,0:T(8,128)S(1)}, u32[]{:S(2)}, u32[]{:S(2)}) collective-permute-start(f32[2,128,512]{2,1,0:T(8,128)S(1)} %get-tuple-element.63), channel_id=1, source_target_pairs={{24,16},{16,8},{8,0},{25,17},{17,9},{9,1},{26,18},{18,10},{10,2},{... | collective-permute-start | bytes 1572872 | tf_op jit(solution)/shard_map/ppermute | solution.py:154
  580.8 14.9 %collective-permute-start.25 = (f32[2,128,512]{2,1,0:T(8,128)S(1)}, f32[2,128,512]{2,1,0:T(8,128)S(1)}, u32[]{:S(2)}, u32[]{:S(2)}) collective-permute-start(f32[2,128,512]{2,1,0:T(8,128)S(1)} %collective-permute-done.24), channel_id=1, source_target_pairs={{16,8},{8,0},{17,9},{9,1},{18,10},{10,2},{19,11},{11,3},{20,12},{1... | collective-permute-start | bytes 1572872 | tf_op jit(solution)/shard_map/ppermute | solution.py:154
  595.9 13.0 %collective-permute-start.26 = (f32[2,128,512]{2,1,0:T(8,128)S(1)}, f32[2,128,512]{2,1,0:T(8,128)S(1)}, u32[]{:S(2)}, u32[]{:S(2)}) collective-permute-start(f32[2,128,512]{2,1,0:T(8,128)S(1)} %multiply_add_fusion.3), channel_id=1, source_target_pairs={{16,0},{17,1},{18,2},{19,3},{20,4},{21,5},{22,6},{23,7}} | collective-permute-start | bytes 1572872 | tf_op jit(solution)/shard_map/ppermute | solution.py:154
  632.3 291.4 %reduce-scatter.5.cloned.1.call-start = ((), (), s32[]{:S(2)}) async-start(), calls=%async_computation.4 | async-start | bytes 10485760 | tf_op jit(solution)/shard_map/reduce_scatter | solution.py:188
  634.7 87.2 %collective-permute-start.38 = (f32[512,2048]{1,0:T(8,128)S(1)}, f32[512,2048]{1,0:T(8,128)S(1)}, u32[]{:S(2)}, u32[]{:S(2)}) collective-permute-start(f32[512,2048]{1,0:T(8,128)S(1)} %convert_reduce-precision_fusion), channel_id=1, source_target_pairs={{0,4},{4,0},{1,5},{5,1},{2,6},{6,2},{3,7},{7,3},{8,12},{12,8},{9,1... | collective-permute-start | bytes 12582920 | tf_op jit(solution)/shard_map/ppermute | solution.py:32
  746.9 26.9 %collective-permute-start.12 = (f32[128,2048]{1,0:T(8,128)S(1)}, f32[128,2048]{1,0:T(8,128)S(1)}, u32[]{:S(2)}, u32[]{:S(2)}) collective-permute-start(f32[128,2048]{1,0:T(8,128)S(1)} %slice.216), channel_id=1, source_target_pairs={{0,2},{1,3},{2,0},{3,1},{4,6},{5,7},{6,4},{7,5},{8,10},{9,11},{10,... | collective-permute-start | bytes 3145736 | tf_op jit(solution)/shard_map/ppermute | solution.py:32
  751.1 45.2 %collective-permute-start.29 = (f32[128,2048]{1,0:T(8,128)S(1)}, f32[128,2048]{1,0:T(8,128)S(1)}, u32[]{:S(2)}, u32[]{:S(2)}) collective-permute-start(f32[128,2048]{1,0:T(8,128)S(1)} %slice.222), channel_id=1, source_target_pairs={{0,2},{1,3},{2,0},{3,1},{4,6},{5,7},{6,4},{7,5},{8,10},{9,11},{10,... | collective-permute-start | bytes 3145736 | tf_op jit(solution)/shard_map/ppermute | solution.py:32
  774.0 44.7 %collective-permute-start.13 = (f32[128,2048]{1,0:T(8,128)S(1)}, f32[128,2048]{1,0:T(8,128)S(1)}, u32[]{:S(2)}, u32[]{:S(2)}) collective-permute-start(f32[128,2048]{1,0:T(8,128)S(1)} %fusion.76), channel_id=1, source_target_pairs={{0,2},{1,3},{2,0},{3,1},{4,6},{5,7},{6,4},{7,5},{8,10},{9,11},{10,... | collective-permute-start | bytes 3145736 | tf_op jit(solution)/shard_map/ppermute | solution.py:32
  797.9 43.1 %collective-permute-start.30 = (f32[128,2048]{1,0:T(8,128)S(1)}, f32[128,2048]{1,0:T(8,128)S(1)}, u32[]{:S(2)}, u32[]{:S(2)}) collective-permute-start(f32[128,2048]{1,0:T(8,128)S(1)} %add_reduce-precision_fusion), channel_id=1, source_target_pairs={{0,2},{1,3},{2,0},{3,1},{4,6},{5,7},{6,4},{7,5},{8,10},{9,11},{10,... | collective-permute-start | bytes 3145736 | tf_op jit(solution)/shard_map/ppermute | solution.py:32
  820.4 30.3 %collective-permute-start.14 = (f32[256,2048]{1,0:T(8,128)}, f32[256,2048]{1,0:T(8,128)}, u32[]{:S(2)}, u32[]{:S(2)}) collective-permute-start(f32[256,2048]{1,0:T(8,128)} %pad_maximum_fusion.4), channel_id=1, source_target_pairs={{0,1},{1,0},{2,3},{3,2},{4,5},{5,4},{6,7},{7,6},{8,9},{9,8},{10,11... | collective-permute-start | bytes 6291464 | tf_op jit(solution)/shard_map/ppermute | solution.py:32
  842.7 20.5 %collective-permute-start.31 = (f32[256,2048]{1,0:T(8,128)}, f32[256,2048]{1,0:T(8,128)}, u32[]{:S(2)}, u32[]{:S(2)}) collective-permute-start(f32[256,2048]{1,0:T(8,128)} %pad_maximum_fusion.9), channel_id=1, source_target_pairs={{0,1},{1,0},{2,3},{3,2},{4,5},{5,4},{6,7},{7,6},{8,9},{9,8},{10,11... | collective-permute-start | bytes 6291464 | tf_op jit(solution)/shard_map/ppermute | solution.py:32
  (114 other events, 2050.0 us)
Sparse Core Ops, SparseCore 0:
  279.5 96.4 reduce-scatter.10
  409.6 175.4 reduce-scatter.8
  632.4 143.4 reduce-scatter.6
  778.1 145.4 reduce-scatter.4

commit v2 on v1

--- a/solution.py
+++ b/solution.py
@@ -1,6 +1,10 @@
+import functools
+
 import jax
 import jax.numpy as jnp
 from jax import lax
+from jax.experimental import pallas as pl
+from jax.experimental.pallas import tpu as pltpu
 from jax.sharding import Mesh
 from jax.sharding import PartitionSpec as P
 
@@ -147,19 +151,11 @@
     step = decay[:, None, None]
     total = step * earlier + later
 
-    def shifted(x, distance, first):
-        moves = [(i, i + distance) for i in range(first, pairs - distance)]
-        if suffix:
-            moves = [(pairs - 1 - i, pairs - 1 - j) for i, j in moves]
-        return lax.ppermute(x, "outer", moves)
-
-    arriving = shifted(total, 1, 0)
-    factor = step * step
-    distance = 1
-    while distance < pairs - 1:
-        arriving = arriving + factor * shifted(arriving, distance, 1)
-        factor = factor * factor
-        distance *= 2
+    arriving = jnp.zeros_like(total)
+    for hop in range(pairs - 1):
+        way = (pairs - 1 - hop, pairs - 2 - hop) if suffix else (hop, hop + 1)
+        leaving = step * step * arriving + total if hop else total
+        arriving = arriving + lax.ppermute(leaving, "outer", [way])
     second = step * arriving + earlier
     mine = jnp.where(odd == 0, arriving, second)
     other = jnp.where(odd == 0, second, arriving)
@@ -171,6 +167,197 @@
     )
 
 
+def scan_kernel(
+    pairs,
+    pieces,
+    decay_ref,
+    rate_ref,
+    local_ref,
+    act_ref,
+    gate_weight_ref,
+    query_ref,
+    key_ref,
+    value_ref,
+    state_ref,
+    gate_ref,
+    weights_ref,
+    intra_ref,
+    got,
+    arriving,
+    leaving,
+    other,
+    rest,
+    give_send,
+    give_recv,
+    chain_send,
+    chain_recv,
+    rest_send,
+    rest_recv,
+):
+    heads, rows, _ = local_ref.shape
+    half = rows // 2
+    count = heads * pieces
+    size = half // pieces
+    outer, odd = lax.axis_index("outer"), lax.axis_index("pair")
+    is_odd = odd == 1
+    has_earlier, has_later = outer > 0, outer < pairs - 1
+    partner = {"pair": 1 - odd}
+
+    barrier = pltpu.get_barrier_semaphore()
+    pl.semaphore_signal(barrier, device_id=partner, device_id_type=pl.DeviceIdType.MESH)
+
+    @pl.when(has_earlier)
+    def _():
+        pl.semaphore_signal(
+            barrier, device_id={"outer": outer - 1}, device_id_type=pl.DeviceIdType.MESH
+        )
+
+    pl.semaphore_wait(barrier, jnp.where(has_later, 2, 1))
+
+    def rows_of(i, which):
+        start = which * half + (i % pieces) * size
+        return i // pieces, pl.ds(pl.multiple_of(start, size), size)
+
+    def give(i):
+        head, place = rows_of(i, 1 - odd)
+        return pltpu.make_async_remote_copy(
+            src_ref=local_ref.at[head, place],
+            dst_ref=got.at[i],
+            send_sem=give_send.at[i],
+            recv_sem=give_recv.at[i],
+            device_id=partner,
+            device_id_type=pl.DeviceIdType.MESH,
+        )
+
+    def onward(i):
+        return pltpu.make_async_remote_copy(
+            src_ref=leaving.at[i],
+            dst_ref=arriving.at[i],
+            send_sem=chain_send.at[i],
+            recv_sem=chain_recv.at[i],
+            device_id={"outer": outer + 1},
+            device_id_type=pl.DeviceIdType.MESH,
+        )
+
+    def finish(i):
+        return pltpu.make_async_remote_copy(
+            src_ref=other.at[i],
+            dst_ref=rest.at[i],
+            send_sem=rest_send.at[i],
+            recv_sem=rest_recv.at[i],
+            device_id=partner,
+            device_id_type=pl.DeviceIdType.MESH,
+        )
+
+    for i in range(count):
+        give(i).start()
+
+    columns = gate_weight_ref.shape[1]
+    tile = columns // 4
+
+    def gate_tile(n):
+        place = pl.ds(n * tile, tile)
+        gate_ref[:, place] = jnp.dot(
+            act_ref[...], gate_weight_ref[:, place], preferred_element_type=F32
+        )
+
+    def scores(h):
+        q = query_ref[:, h * KD : (h + 1) * KD]
+        k = key_ref[:, h * KD : (h + 1) * KD]
+        length = q.shape[0]
+        value = times_transpose(q, k)
+        place = lax.broadcasted_iota(jnp.int32, (length, length), 0)
+        place = place - lax.broadcasted_iota(jnp.int32, (length, length), 1)
+        fading = jnp.exp(-rate_ref[h] * jnp.maximum(place, 0).astype(F32))
+        weights_ref[h] = jnp.where(place >= 0, value * fading, 0.0).astype(BF16)
+
+    def intra(h):
+        intra_ref[h] = jnp.dot(
+            weights_ref[h], value_ref[:, h * VD : (h + 1) * VD], preferred_element_type=F32
+        )
+
+    work = [functools.partial(gate_tile, n) for n in range(4)]
+    for h in range(heads):
+        work.append(functools.partial(scores, h))
+        work.append(functools.partial(intra, h))
+    per_piece = -(-(len(work) - 2) // count)
+    for job in work[:2]:
+        job()
+    work = work[2:]
+
+    for i in range(count):
+        head, kept_rows = rows_of(i, odd)
+        give(i).wait_recv()
+        kept, came = local_ref[head, kept_rows], got[i]
+        earlier = jnp.where(is_odd, came, kept)
+        later = jnp.where(is_odd, kept, came)
+        decay = decay_ref[head]
+
+        @pl.when(has_earlier)
+        def _():
+            onward(i).wait_recv()
+
+        @pl.when(jnp.logical_not(has_earlier))
+        def _():
+            arriving[i] = jnp.zeros_like(came)
+
+        state = arriving[i]
+        second = decay * state + earlier
+
+        @pl.when(has_later)
+        def _():
+            leaving[i] = decay * second + later
+            onward(i).start()
+
+        other[i] = jnp.where(is_odd, state, second)
+        finish(i).start()
+        state_ref[head, kept_rows] = jnp.where(is_odd, second, state)
+        for job in work[:per_piece]:
+            job()
+        work = work[per_piece:]
+    for i in range(count):
+        head, place = rows_of(i, 1 - odd)
+        finish(i).wait_recv()
+        state_ref[head, place] = rest[i]
+    for i in range(count):
+        give(i).wait_send()
+        finish(i).wait_send()
+
+        @pl.when(has_later)
+        def _():
+            onward(i).wait_send()
+
+
+def scan_states(local, decay, rate, act, gate_weight, queries, key_rows, value_rows):
+    heads, rows, columns = local.shape
+    length = act.shape[0]
+    pieces = 2
+    count = heads * pieces
+    buffer = pltpu.VMEM((count, rows // 2 // pieces, columns), F32)
+    vector = pl.BlockSpec(memory_space=pltpu.VMEM)
+    scalar = pl.BlockSpec(memory_space=pltpu.SMEM)
+    return pl.pallas_call(
+        functools.partial(scan_kernel, lax.axis_size("outer"), pieces),
+        out_shape=(
+            jax.ShapeDtypeStruct(local.shape, F32),
+            jax.ShapeDtypeStruct((length, gate_weight.shape[1]), F32),
+            jax.ShapeDtypeStruct((heads, length, length), BF16),
+            jax.ShapeDtypeStruct((heads, length, VD), F32),
+        ),
+        in_specs=[scalar, scalar] + [vector] * 6,
+        out_specs=(vector,) * 4,
+        scratch_shapes=[buffer] * 5 + [pltpu.SemaphoreType.DMA((count,))] * 6,
+        compiler_params=pltpu.CompilerParams(
+            collective_id=0, has_side_effects=True, vmem_limit_bytes=40 * 1024 * 1024
+        ),
+        cost_estimate=pl.CostEstimate(
+            flops=2 * length * act.shape[1] * gate_weight.shape[1],
+            bytes_accessed=16 * 1024 * 1024,
+            transcendentals=heads * length * length,
+        ),
+    )(decay, rate, local, act, gate_weight, queries, key_rows, value_rows)
+
+
 def split_columns(x):
     outer, place = lax.axis_size("outer"), lax.axis_index("pair")
     size = x.shape[1] // (2 * outer)
@@ -184,8 +371,8 @@
     return blocks(place), blocks(1 - place)
 
 
-def sum_blocks(x, dim):
-    return lax.psum_scatter(x, "outer", scatter_dimension=dim, tiled=True)
+def sum_blocks(x):
+    return lax.psum_scatter(x, "outer", scatter_dimension=0, tiled=True)
 
 
 def shards(
@@ -234,15 +421,22 @@
             for h in head_range
         ]
     )
-    state_in = carry_states(local_state, block_decay, False)
-
-    gate_pre = dot(first_act, gate_weight)
+    state_in, gate_pre, retain_weights, intra = scan_states(
+        local_state,
+        block_decay,
+        decay_rate,
+        first_act,
+        gate_weight,
+        queries,
+        key_rows,
+        value_rows,
+    )
+
     sigmoid_gate = jax.nn.sigmoid(gate_pre)
     swish_gate = gate_pre * sigmoid_gate
-    retain_weights = [(times_transpose(q[h], k[h]) * masks[h]).astype(BF16) for h in head_range]
     group_normed, spread = [], []
     for h in head_range:
-        retained = dot(retain_weights[h], v[h]) + fade_in[h] * jnp.dot(
+        retained = intra[h] + fade_in[h] * jnp.dot(
             q[h].astype(F32), state_in[h], precision=FULL_ACCURACY
         )
         centred = retained - jnp.mean(retained, axis=-1, keepdims=True)
@@ -282,10 +476,10 @@
     mlp_pre_grad = (product_grad * up_pre * gelu_slope).astype(BF16)
     mlp_grads = jnp.concatenate([up_pre_grad, mlp_pre_grad], axis=1)
     mlp_given = flip(widen(mlp_grads), "pair", 1)
-    second_act_grad = scatter_rows(
-        times_transpose(up_pre_grad, up_weight) + times_transpose(mlp_pre_grad, mlp_gate_weight),
-        "head",
-    )
+    second_act_grad = times_transpose(up_pre_grad, up_weight) + times_transpose(
+        mlp_pre_grad, mlp_gate_weight
+    )
+    second_act_grad = scatter_rows(second_act_grad, "head")
     hidden_grad = cot_rows + norm_back(
         second_act_grad * second_scale, second_normed, second_inverse
     )
@@ -294,7 +488,7 @@
 
     product_pair = jnp.concatenate([product, narrow(after(product_given, cast_rows), zero)])
     down_term = contract_rows(cot_pair, product_pair)
-    down_grad = sum_blocks(down_term, 0).T
+    down_grad = sum_blocks(down_term).T
 
     hidden_cast = from_relative(narrow(after(cast_all, down_term), zero), "head", 0)
     gated_grad = times_transpose(hidden_cast, output_weight)
@@ -323,10 +517,10 @@
     second_pair = jnp.concatenate([split_columns(second_act)[0], second_given])
     mlp_pair = jnp.concatenate([mlp_grads, narrow(after(mlp_given, state_term), zero)])
     mlp_term = contract_rows(second_pair, mlp_pair)
-    up_both = sum_blocks(mlp_term, 0)
+    mlp_both = sum_blocks(mlp_term)
+    hidden_units = up_weight.shape[1]
+    up_grad, mlp_gate_grad = mlp_both[:, :hidden_units], mlp_both[:, hidden_units:]
     state_grad = carry_states(state_term, block_decay, True, mlp_term)
-    hidden_units = up_weight.shape[1]
-    up_grad, mlp_gate_grad = up_both[:, :hidden_units], up_both[:, hidden_units:]
 
     output_rows = hidden + scatter_rows(dot(product, after(down_weight, cast_rows)), "head")
     output_rows = widen(output_rows)
@@ -358,17 +552,17 @@
     cast_given = from_relative(narrow(gather_rows(cast_given, "head"), zero), "head", 0)
     cast_pair = jnp.concatenate([split_columns(hidden_cast)[0], cast_given])
     gated_pair = jnp.concatenate([gated_rows, narrow(gated_given, zero)])
-    first_pair = jnp.concatenate([first_kept, narrow(after(first_given, head_grads), zero)])
+    first_pair = jnp.concatenate([first_kept, narrow(first_given, zero)])
     gate_pair = jnp.concatenate([gate_pre_grad, narrow(gate_given, zero)])
     output_term = jnp.concatenate(
         [contract_rows(cast_pair, gated_pair), contract_rows(first_pair, gate_pair)], axis=1
     )
-    output_both = sum_blocks(output_term, 0)
+    output_both = sum_blocks(output_term)
     output_columns = gated_rows.shape[1]
     output_grad, gate_grad = output_both[:, :output_columns].T, output_both[:, output_columns:]
 
     head_pair = jnp.concatenate([head_grads, narrow(after(head_given, output_term), zero)])
-    head_both = sum_blocks(contract_rows(first_pair, head_pair), 0)
+    head_both = sum_blocks(contract_rows(first_pair, head_pair))
     key_columns, value_columns = local_heads * KD, 2 * local_heads * KD
     query_grad = head_both[:, :key_columns]
     key_grad = head_both[:, key_columns:value_columns]

time: 942 us -> 986 us (1.047)
  waiting for transfers between devices: 653 us -> 699 us
  Pallas kernels: 0 us -> 29.9 us
  starting transfers between devices: 53.9 us -> 34.5 us
  matrix products: 105 us -> 93.7 us
    ppermute x38 -> x36, waiting for transfers between devices: 531 us -> 587 us  [flip(): return lax.ppermute(x, axis, [(i, i ^ bit) for i in range(count)])]
    reduce_scatter x4, waiting for transfers between devices: 49.3 us -> 0.01 us  [sum_blocks(): return lax.psum_scatter(x, 'outer', scatter_dimension=0, tiled=True)]
    ppermute x6 -> x3, waiting for transfers between devices: 72.9 us -> 113 us  [carry_states(): arriving = arriving + lax.ppermute(leaving, 'outer', [way])]
    pallas_call x0 -> x1, Pallas kernels: none -> 29.9 us  [scan_states(): pl.pallas_call(functools.partial(scan_kernel, lax.axis_size('outer'), pie...]
    ppermute x38 -> x36, starting transfers between devices: 42 us -> 30.9 us  [flip(): return lax.ppermute(x, axis, [(i, i ^ bit) for i in range(count)])]
    dot_general x12 -> x9, matrix products: 40.7 us -> 30.6 us  [dot(): return jnp.dot(a, b, preferred_element_type=F32)]
    dot_general x16 -> x14, matrix products: 28.4 us -> 28.8 us  [times_transpose(): lax.dot_general(left_side, right_side, (((1,), (1,)), ((), ())), precisio...]
  transfers between devices with their start and end apart: 48 -> 43, of which waited for: 31 -> 28; matrix products, arithmetic and copies ran while one was open for 14% -> 12% of each run, Pallas kernels for 0% -> 0%
where the time goes in v2:
time: 986 us; the launch traced here: 978 us
  waiting for transfers between devices  699 us (71%)
  matrix products  93.7 us (10%)
  other arithmetic  65 us (7%)
  local copies, waits for them, and re-layouts  37.4 us (4%)
  starting transfers between devices  34.5 us (3%)
  Pallas kernels  29.9 us (3%)
  between operations  18 us (2%)
    ppermute x36, waiting for transfers between devices, flip(): return lax.ppermute(x, axis, [(i, i ^ bit) for i in range(count)])  587 us
    ppermute x3, waiting for transfers between devices, carry_states(): arriving = arriving + lax.ppermute(leaving, 'outer', [way])  113 us
    ppermute x36, starting transfers between devices, flip(): return lax.ppermute(x, axis, [(i, i ^ bit) for i in range(count)])  30.9 us
    dot_general x9, matrix products, dot(): return jnp.dot(a, b, preferred_element_type=F32)  30.6 us
    pallas_call x1, Pallas kernels, scan_states(): pl.pallas_call(functools.partial(scan_kernel, lax.axis_size('outer'), pie...  29.9 us
    dot_general x13, matrix products, contract_rows(): lax.dot_general(left_side, right_side, (((0,), (0,)), ((), ())), precisio...  29.7 us
    dot_general x14, matrix products, times_transpose(): lax.dot_general(left_side, right_side, (((1,), (1,)), ((), ())), precisio...  28.8 us
  transfers between devices with their start and end apart: 43, of which 28 were waited for; matrix products, arithmetic and copies ran while one was open for 12% of the time, Pallas kernels for 0%

profile of v2, /device:TPU:0, one launch (start us, length us, event | category | flops | bytes accessed | tf_op | source)
XLA Modules:
  0.0 977.9 jit_solution(1597872564674491091)
XLA Ops:
  24.3 29.9 %shard_map.254 = (f32[2,256,512]{2,1,0:T(8,128)S(1)}, f32[512,1024]{1,0:T(8,128)S(1)}, bf16[2,512,512]{2,1,0:T(8,128)(2,1)S(1)}, f32[2,512,512]{2,1,0:T(8,128)S(1)}) custom-call(f32[2]{0:T(128)S(1)} %get-tuple-element.174.decay_ref, f32[2]{0:T(128)S(1)} %copy-done.13, f32[2,256,512]{2,1,0:T(8,128)S(1)} %pad_maximum_fusion.14.local_ref, ...), custom_call_target="tpu_custom_call" | custom-call | flops 2147483648 | bytes 16777216 | tf_op jit(solution)/shard_map/pallas_call | solution.py:339
  59.0 4.0 fusion.76
  65.7 4.1 collective-permute-done
  72.5 23.1 %collective-permute-done.1 = f32[128,2048]{1,0:T(8,128)S(1)} collective-permute-done((f32[128,2048]{1,0:T(8,128)S(1)}, f32[128,2048]{1,0:T(8,128)S(1)}, u32[]{:S(2)}, u32[]{:S(2)}) %collective-permute-start.1) | collective-permute-done | bytes 1048608 | tf_op jit(solution)/shard_map/ppermute | solution.py:36
  98.7 22.8 %collective-permute-done.2 = f32[128,2048]{1,0:T(8,128)S(1)} collective-permute-done((f32[128,2048]{1,0:T(8,128)S(1)}, f32[128,2048]{1,0:T(8,128)S(1)}, u32[]{:S(2)}, u32[]{:S(2)}) %collective-permute-start.2) | collective-permute-done | bytes 1048608 | tf_op jit(solution)/shard_map/ppermute | solution.py:36
  134.9 15.9 %convert_reduce-precision_fusion.5 = (f32[512,1024]{1,0:T(8,128)}, bf16[512,1024]{1,0:T(8,128)(2,1)}, bf16[512,1024]{1,0:T(8,128)(2,1)S(1)}, bf16[512,1024]{1,0:T(8,128)(2,1)S(1)}) fusion(f32[512,1024]{1,0:T(8,128)S(1)} %fusion.179, f32[512,1024]{1,0:T(8,128)S(1)} %fusion.167, bf16[512,2048]{1,0:T(8,128)(2,1)S(1)} %fusion, bf16[2048,1024]{1,0:T(8,128)(2,1)S(1)} %copy-done.87), kind=kOutput, calls=%fused_computation.97 | convolution fusion | flops 2156920832 | bytes 15728640 | tf_op jit(solution)/shard_map/dot_general | solution.py:112
  167.2 42.6 %collective-permute-done.12 = f32[512,1024]{1,0:T(8,128)S(1)} collective-permute-done((f32[512,1024]{1,0:T(8,128)S(1)}, f32[512,1024]{1,0:T(8,128)S(1)}, u32[]{:S(2)}, u32[]{:S(2)}) %collective-permute-start.12) | collective-permute-done | bytes 2097184 | tf_op jit(solution)/shard_map/ppermute | solution.py:36
  213.0 40.8 %collective-permute-done.13 = f32[512,1024]{1,0:T(8,128)S(1)} collective-permute-done((f32[512,1024]{1,0:T(8,128)S(1)}, f32[512,1024]{1,0:T(8,128)S(1)}, u32[]{:S(2)}, u32[]{:S(2)}) %collective-permute-start.13) | collective-permute-done | bytes 2097184 | tf_op jit(solution)/shard_map/ppermute | solution.py:36
  254.0 4.4 fusion.19
  262.9 100.7 %collective-permute-done.15 = f32[128,1024]{1,0:T(8,128)S(1)} collective-permute-done((f32[128,1024]{1,0:T(8,128)S(1)}, f32[128,1024]{1,0:T(8,128)S(1)}, u32[]{:S(2)}, u32[]{:S(2)}) %collective-permute-start.15) | collective-permute-done | bytes 524320 | tf_op jit(solution)/shard_map/ppermute | solution.py:36
  365.1 10.6 %collective-permute-done.16 = f32[128,1024]{1,0:T(8,128)S(1)} collective-permute-done((f32[128,1024]{1,0:T(8,128)S(1)}, f32[128,1024]{1,0:T(8,128)S(1)}, u32[]{:S(2)}, u32[]{:S(2)}) %collective-permute-start.16) | collective-permute-done | bytes 524320 | tf_op jit(solution)/shard_map/ppermute | solution.py:36
  380.5 8.0 fusion.2
  390.5 23.9 %collective-permute-done.10 = f32[128,2048]{1,0:T(8,128)S(1)} collective-permute-done((f32[128,2048]{1,0:T(8,128)}, f32[128,2048]{1,0:T(8,128)S(1)}, u32[]{:S(2)}, u32[]{:S(2)}) %collective-permute-start.10) | collective-permute-done | bytes 1048608 | tf_op jit(solution)/shard_map/ppermute | solution.py:36
  414.4 3.2 pad_maximum_fusion.6
  418.4 13.9 %collective-permute-done.34 = f32[128,1024]{1,0:T(8,128)} collective-permute-done((f32[128,1024]{1,0:T(8,128)S(1)}, f32[128,1024]{1,0:T(8,128)}, u32[]{:S(2)}, u32[]{:S(2)}) %collective-permute-start.34) | collective-permute-done | bytes 524320 | tf_op jit(solution)/shard_map/ppermute | solution.py:36
  438.4 7.6 collective-permute-done.35
  452.5 8.2 convert_reduce-precision_fusion.2
  461.2 23.7 %collective-permute-done.32 = f32[512,1024]{1,0:T(8,128)S(1)} collective-permute-done((f32[512,1024]{1,0:T(8,128)S(1)}, f32[512,1024]{1,0:T(8,128)S(1)}, u32[]{:S(2)}, u32[]{:S(2)}) %collective-permute-start.32) | collective-permute-done | bytes 2097184 | tf_op jit(solution)/shard_map/ppermute | solution.py:36
  487.0 42.8 %collective-permute-done.37 = f32[512,1024]{1,0:T(8,128)S(1)} collective-permute-done((f32[512,1024]{1,0:T(8,128)S(1)}, f32[512,1024]{1,0:T(8,128)S(1)}, u32[]{:S(2)}, u32[]{:S(2)}) %collective-permute-start.37) | collective-permute-done | bytes 2097184 | tf_op jit(solution)/shard_map/ppermute | solution.py:36
  534.1 39.1 %collective-permute-done.38 = f32[512,1024]{1,0:T(8,128)S(1)} collective-permute-done((f32[512,1024]{1,0:T(8,128)}, f32[512,1024]{1,0:T(8,128)S(1)}, u32[]{:S(2)}, u32[]{:S(2)}) %collective-permute-start.38) | collective-permute-done | bytes 2097184 | tf_op jit(solution)/shard_map/ppermute | solution.py:36
  576.0 4.2 pad_maximum_fusion
  589.6 10.5 %collective-permute-done.14 = f32[2,128,512]{2,1,0:T(8,128)S(1)} collective-permute-done((f32[2,128,512]{2,1,0:T(8,128)S(1)}, f32[2,128,512]{2,1,0:T(8,128)S(1)}, u32[]{:S(2)}, u32[]{:S(2)}) %collective-permute-start.14) | collective-permute-done | bytes 524320 | tf_op jit(solution)/shard_map/ppermute | solution.py:36
  606.9 112.7 %collective-permute-done.21 = f32[2,128,512]{2,1,0:T(8,128)S(1)} collective-permute-done((f32[2,128,512]{2,1,0:T(8,128)S(1)}, f32[2,128,512]{2,1,0:T(8,128)S(1)}, u32[]{:S(2)}, u32[]{:S(2)}) %collective-permute-start.21) | collective-permute-done | bytes 524320 | tf_op jit(solution)/shard_map/ppermute | solution.py:158
  723.1 11.6 %collective-permute-done.22 = f32[2,128,512]{2,1,0:T(8,128)S(1)} collective-permute-done((f32[2,128,512]{2,1,0:T(8,128)S(1)}, f32[2,128,512]{2,1,0:T(8,128)S(1)}, u32[]{:S(2)}, u32[]{:S(2)}) %collective-permute-start.22) | collective-permute-done | bytes 524320 | tf_op jit(solution)/shard_map/ppermute | solution.py:36
  741.9 73.6 %collective-permute-done.33 = f32[512,2048]{1,0:T(8,128)S(1)} collective-permute-done((f32[512,2048]{1,0:T(8,128)S(1)}, f32[512,2048]{1,0:T(8,128)S(1)}, u32[]{:S(2)}, u32[]{:S(2)}) %collective-permute-start.33) | collective-permute-done | bytes 4194336 | tf_op jit(solution)/shard_map/ppermute | solution.py:36
  816.1 8.0 fusion.9
  825.2 4.5 fusion.181
  847.3 19.5 %collective-permute-done.7 = f32[128,2048]{1,0:T(8,128)S(1)} collective-permute-done((f32[128,2048]{1,0:T(8,128)S(1)}, f32[128,2048]{1,0:T(8,128)S(1)}, u32[]{:S(2)}, u32[]{:S(2)}) %collective-permute-start.7) | collective-permute-done | bytes 1048608 | tf_op jit(solution)/shard_map/ppermute | solution.py:36
  868.8 20.5 %collective-permute-done.24 = f32[128,2048]{1,0:T(8,128)S(1)} collective-permute-done((f32[128,2048]{1,0:T(8,128)S(1)}, f32[128,2048]{1,0:T(8,128)S(1)}, u32[]{:S(2)}, u32[]{:S(2)}) %collective-permute-start.24) | collective-permute-done | bytes 1048608 | tf_op jit(solution)/shard_map/ppermute | solution.py:36
  892.7 19.1 %collective-permute-done.8 = f32[128,2048]{1,0:T(8,128)S(1)} collective-permute-done((f32[128,2048]{1,0:T(8,128)S(1)}, f32[128,2048]{1,0:T(8,128)S(1)}, u32[]{:S(2)}, u32[]{:S(2)}) %collective-permute-start.8) | collective-permute-done | bytes 1048608 | tf_op jit(solution)/shard_map/ppermute | solution.py:36
  913.5 20.3 %collective-permute-done.25 = f32[128,2048]{1,0:T(8,128)S(1)} collective-permute-done((f32[128,2048]{1,0:T(8,128)S(1)}, f32[128,2048]{1,0:T(8,128)S(1)}, u32[]{:S(2)}, u32[]{:S(2)}) %collective-permute-start.25) | collective-permute-done | bytes 1048608 | tf_op jit(solution)/shard_map/ppermute | solution.py:36
  939.4 4.0 collective-permute-done.28
  (421 shorter events, 182.0 us)
Async XLA Ops:
  7.2 946.0 %reduce-scatter.11.cloned.1.call-start = ((), (), s32[]{:S(2)}) async-start(), calls=%async_computation.7 | async-start | bytes 5242880 | tf_op jit(solution)/shard_map/reduce_scatter | solution.py:375
  70.3 25.3 %collective-permute-start.1 = (f32[128,2048]{1,0:T(8,128)S(1)}, f32[128,2048]{1,0:T(8,128)S(1)}, u32[]{:S(2)}, u32[]{:S(2)}) collective-permute-start(f32[128,2048]{1,0:T(8,128)S(1)} %slice.222), channel_id=1, source_target_pairs={{0,2},{1,3},{2,0},{3,1},{4,6},{5,7},{6,4},{7,5},{8,10},{9,11},{10,... | collective-permute-start | bytes 3145736 | tf_op jit(solution)/shard_map/ppermute | solution.py:36
  97.1 24.4 %collective-permute-start.2 = (f32[128,2048]{1,0:T(8,128)S(1)}, f32[128,2048]{1,0:T(8,128)S(1)}, u32[]{:S(2)}, u32[]{:S(2)}) collective-permute-start(f32[128,2048]{1,0:T(8,128)S(1)} %add_reduce-precision_fusion.1), channel_id=1, source_target_pairs={{0,2},{1,3},{2,0},{3,1},{4,6},{5,7},{6,4},{7,5},{8,10},{9,11},{10,... | collective-permute-start | bytes 3145736 | tf_op jit(solution)/shard_map/ppermute | solution.py:36
  123.2 6.0 collective-permute-start.3
  161.2 48.6 %collective-permute-start.12 = (f32[512,1024]{1,0:T(8,128)S(1)}, f32[512,1024]{1,0:T(8,128)S(1)}, u32[]{:S(2)}, u32[]{:S(2)}) collective-permute-start(f32[512,1024]{1,0:T(8,128)S(1)} %convert_reduce-precision_fusion.6), channel_id=1, source_target_pairs={{0,4},{4,0},{1,5},{5,1},{2,6},{6,2},{3,7},{7,3},{8,12},{12,8},{9,1... | collective-permute-start | bytes 6291464 | tf_op jit(solution)/shard_map/ppermute | solution.py:36
  165.1 45.0 %collective-permute-start.5 = (f32[128,2048]{1,0:T(8,128)S(1)}, f32[128,2048]{1,0:T(8,128)S(1)}, u32[]{:S(2)}, u32[]{:S(2)}) collective-permute-start(f32[128,2048]{1,0:T(8,128)S(1)} %slice.226), channel_id=1, source_target_pairs={{0,2},{1,3},{2,0},{3,1},{4,6},{5,7},{6,4},{7,5},{8,10},{9,11},{10,... | collective-permute-start | bytes 3145736 | tf_op jit(solution)/shard_map/ppermute | solution.py:36
  166.7 87.1 %collective-permute-start.13 = (f32[512,1024]{1,0:T(8,128)S(1)}, f32[512,1024]{1,0:T(8,128)S(1)}, u32[]{:S(2)}, u32[]{:S(2)}) collective-permute-start(f32[512,1024]{1,0:T(8,128)S(1)} %copy-done.93), channel_id=1, source_target_pairs={{0,4},{4,0},{1,5},{5,1},{2,6},{6,2},{3,7},{7,3},{8,12},{12,8},{9,1... | collective-permute-start | bytes 6291464 | tf_op jit(solution)/shard_map/ppermute | solution.py:36
  258.4 702.0 %reduce-scatter.9.cloned.1.call-start = ((), (), s32[]{:S(2)}) async-start(), calls=%async_computation.6 | async-start | bytes 10485760 | tf_op jit(solution)/shard_map/reduce_scatter | solution.py:375
  260.7 118.3 %collective-permute-start.18 = (f32[512,2048]{1,0:T(8,128)S(1)}, f32[512,2048]{1,0:T(8,128)S(1)}, u32[]{:S(2)}, u32[]{:S(2)}) collective-permute-start(f32[512,2048]{1,0:T(8,128)S(1)} %convert_reduce-precision_fusion.1), channel_id=1, source_target_pairs={{0,4},{4,0},{1,5},{5,1},{2,6},{6,2},{3,7},{7,3},{8,12},{12,8},{9,1... | collective-permute-start | bytes 12582920 | tf_op jit(solution)/shard_map/ppermute | solution.py:36
  261.4 102.2 %collective-permute-start.15 = (f32[128,1024]{1,0:T(8,128)S(1)}, f32[128,1024]{1,0:T(8,128)S(1)}, u32[]{:S(2)}, u32[]{:S(2)}) collective-permute-start(f32[128,1024]{1,0:T(8,128)S(1)} %pad_maximum_fusion.18), channel_id=1, source_target_pairs={{0,4},{4,0},{1,5},{5,1},{2,6},{6,2},{3,7},{7,3},{8,12},{12,8},{9,1... | collective-permute-start | bytes 1572872 | tf_op jit(solution)/shard_map/ppermute | solution.py:36
  363.6 12.1 %collective-permute-start.16 = (f32[128,1024]{1,0:T(8,128)S(1)}, f32[128,1024]{1,0:T(8,128)S(1)}, u32[]{:S(2)}, u32[]{:S(2)}) collective-permute-start(f32[128,1024]{1,0:T(8,128)S(1)} %collective-permute-done.15), channel_id=1, source_target_pairs={{0,2},{1,3},{2,0},{3,1},{4,6},{5,7},{6,4},{7,5},{8,10},{9,11},{10,... | collective-permute-start | bytes 1572872 | tf_op jit(solution)/shard_map/ppermute | solution.py:36
  388.5 575.1 %reduce-scatter.7.cloned.1.call-start = ((), (), s32[]{:S(2)}) async-start(), calls=%async_computation.5 | async-start | bytes 10485760 | tf_op jit(solution)/shard_map/reduce_scatter | solution.py:375
  388.9 25.5 %collective-permute-start.10 = (f32[128,2048]{1,0:T(8,128)}, f32[128,2048]{1,0:T(8,128)S(1)}, u32[]{:S(2)}, u32[]{:S(2)}) collective-permute-start(f32[128,2048]{1,0:T(8,128)} %get-tuple-element.75), channel_id=1, source_target_pairs={{0,2},{1,3},{2,0},{3,1},{4,6},{5,7},{6,4},{7,5},{8,10},{9,11},{10,... | collective-permute-start | bytes 3145736 | tf_op jit(solution)/shard_map/ppermute | solution.py:36
  417.7 29.8 %collective-permute-start.11 = (f32[256,2048]{1,0:T(8,128)}, f32[256,2048]{1,0:T(8,128)}, u32[]{:S(2)}, u32[]{:S(2)}) collective-permute-start(f32[256,2048]{1,0:T(8,128)} %pad_maximum_fusion.6), channel_id=1, source_target_pairs={{0,1},{1,0},{2,3},{3,2},{4,5},{5,4},{6,7},{7,6},{8,9},{9,8},{10,11... | collective-permute-start | bytes 6291464 | tf_op jit(solution)/shard_map/ppermute | solution.py:36
  417.8 14.5 %collective-permute-start.34 = (f32[128,1024]{1,0:T(8,128)S(1)}, f32[128,1024]{1,0:T(8,128)}, u32[]{:S(2)}, u32[]{:S(2)}) collective-permute-start(f32[128,1024]{1,0:T(8,128)S(1)} %pad_maximum_fusion.19), channel_id=1, source_target_pairs={{0,4},{4,0},{1,5},{5,1},{2,6},{6,2},{3,7},{7,3},{8,12},{12,8},{9,1... | collective-permute-start | bytes 1572872 | tf_op jit(solution)/shard_map/ppermute | solution.py:36
  432.3 13.8 %collective-permute-start.35 = (f32[128,1024]{1,0:T(8,128)}, f32[128,1024]{1,0:T(8,128)}, u32[]{:S(2)}, u32[]{:S(2)}) collective-permute-start(f32[128,1024]{1,0:T(8,128)} %collective-permute-done.34), channel_id=1, source_target_pairs={{0,2},{1,3},{2,0},{3,1},{4,6},{5,7},{6,4},{7,5},{8,10},{9,11},{10,... | collective-permute-start | bytes 1572872 | tf_op jit(solution)/shard_map/ppermute | solution.py:36
  436.3 48.6 %collective-permute-start.32 = (f32[512,1024]{1,0:T(8,128)S(1)}, f32[512,1024]{1,0:T(8,128)S(1)}, u32[]{:S(2)}, u32[]{:S(2)}) collective-permute-start(f32[512,1024]{1,0:T(8,128)S(1)} %convert_reduce-precision_fusion.4), channel_id=1, source_target_pairs={{0,4},{4,0},{1,5},{5,1},{2,6},{6,2},{3,7},{7,3},{8,12},{12,8},{9,1... | collective-permute-start | bytes 6291464 | tf_op jit(solution)/shard_map/ppermute | solution.py:36
  436.9 92.9 %collective-permute-start.37 = (f32[512,1024]{1,0:T(8,128)S(1)}, f32[512,1024]{1,0:T(8,128)S(1)}, u32[]{:S(2)}, u32[]{:S(2)}) collective-permute-start(f32[512,1024]{1,0:T(8,128)S(1)} %convert_reduce-precision_fusion.3), channel_id=1, source_target_pairs={{0,4},{4,0},{1,5},{5,1},{2,6},{6,2},{3,7},{7,3},{8,12},{12,8},{9,1... | collective-permute-start | bytes 6291464 | tf_op jit(solution)/shard_map/ppermute | solution.py:36
  447.4 37.8 %collective-permute-start.36 = (f32[256,1024]{1,0:T(8,128)S(1)}, f32[256,1024]{1,0:T(8,128)S(1)}, u32[]{:S(2)}, u32[]{:S(2)}) collective-permute-start(f32[256,1024]{1,0:T(8,128)S(1)} %pad_maximum_fusion.17), channel_id=1, source_target_pairs={{0,1},{1,0},{2,3},{3,2},{4,5},{5,4},{6,7},{7,6},{8,9},{9,8},{10,11... | collective-permute-start | bytes 3145736 | tf_op jit(solution)/shard_map/ppermute | solution.py:36
  460.6 112.5 %collective-permute-start.38 = (f32[512,1024]{1,0:T(8,128)}, f32[512,1024]{1,0:T(8,128)S(1)}, u32[]{:S(2)}, u32[]{:S(2)}) collective-permute-start(f32[512,1024]{1,0:T(8,128)} %get-tuple-element.66), channel_id=1, source_target_pairs={{0,4},{4,0},{1,5},{5,1},{2,6},{6,2},{3,7},{7,3},{8,12},{12,8},{9,1... | collective-permute-start | bytes 6291464 | tf_op jit(solution)/shard_map/ppermute | solution.py:36
  580.1 387.4 %reduce-scatter.5.cloned.1.call-start = ((), (), s32[]{:S(2)}) async-start(), calls=%async_computation.4 | async-start | bytes 10485760 | tf_op jit(solution)/shard_map/reduce_scatter | solution.py:375
  587.7 12.4 %collective-permute-start.14 = (f32[2,128,512]{2,1,0:T(8,128)S(1)}, f32[2,128,512]{2,1,0:T(8,128)S(1)}, u32[]{:S(2)}, u32[]{:S(2)}) collective-permute-start(f32[2,128,512]{2,1,0:T(8,128)S(1)} %fusion.93), channel_id=1, source_target_pairs={{0,4},{4,0},{1,5},{5,1},{2,6},{6,2},{3,7},{7,3},{8,12},{12,8},{9,1... | collective-permute-start | bytes 1572872 | tf_op jit(solution)/shard_map/ppermute | solution.py:36
  603.8 115.8 %collective-permute-start.21 = (f32[2,128,512]{2,1,0:T(8,128)S(1)}, f32[2,128,512]{2,1,0:T(8,128)S(1)}, u32[]{:S(2)}, u32[]{:S(2)}) collective-permute-start(f32[2,128,512]{2,1,0:T(8,128)S(1)} %get-tuple-element.69), channel_id=1, source_target_pairs={{8,0},{9,1},{10,2},{11,3},{12,4},{13,5},{14,6},{15,7}} | collective-permute-start | bytes 1572872 | tf_op jit(solution)/shard_map/ppermute | solution.py:158
  719.8 14.9 %collective-permute-start.22 = (f32[2,128,512]{2,1,0:T(8,128)S(1)}, f32[2,128,512]{2,1,0:T(8,128)S(1)}, u32[]{:S(2)}, u32[]{:S(2)}) collective-permute-start(f32[2,128,512]{2,1,0:T(8,128)S(1)} %get-tuple-element.93), channel_id=1, source_target_pairs={{0,4},{4,0},{1,5},{5,1},{2,6},{6,2},{3,7},{7,3},{8,12},{12,8},{9,1... | collective-permute-start | bytes 1572872 | tf_op jit(solution)/shard_map/ppermute | solution.py:36
  740.4 75.2 %collective-permute-start.33 = (f32[512,2048]{1,0:T(8,128)S(1)}, f32[512,2048]{1,0:T(8,128)S(1)}, u32[]{:S(2)}, u32[]{:S(2)}) collective-permute-start(f32[512,2048]{1,0:T(8,128)S(1)} %convert_reduce-precision_fusion), channel_id=1, source_target_pairs={{0,4},{4,0},{1,5},{5,1},{2,6},{6,2},{3,7},{7,3},{8,12},{12,8},{9,1... | collective-permute-start | bytes 12582920 | tf_op jit(solution)/shard_map/ppermute | solution.py:36
  830.0 10.3 %collective-permute-start.6 = (f32[256,2048]{1,0:T(8,128)S(1)}, f32[256,2048]{1,0:T(8,128)S(1)}, u32[]{:S(2)}, u32[]{:S(2)}) collective-permute-start(f32[256,2048]{1,0:T(8,128)S(1)} %slice.228), channel_id=1, source_target_pairs={{0,1},{1,0},{2,3},{3,2},{4,5},{5,4},{6,7},{7,6},{8,9},{9,8},{10,11... | collective-permute-start | bytes 6291464 | tf_op jit(solution)/shard_map/ppermute | solution.py:36
  840.8 26.1 %collective-permute-start.7 = (f32[128,2048]{1,0:T(8,128)S(1)}, f32[128,2048]{1,0:T(8,128)S(1)}, u32[]{:S(2)}, u32[]{:S(2)}) collective-permute-start(f32[128,2048]{1,0:T(8,128)S(1)} %slice.230), channel_id=1, source_target_pairs={{0,2},{1,3},{2,0},{3,1},{4,6},{5,7},{6,4},{7,5},{8,10},{9,11},{10,... | collective-permute-start | bytes 3145736 | tf_op jit(solution)/shard_map/ppermute | solution.py:36
  844.9 44.5 %collective-permute-start.24 = (f32[128,2048]{1,0:T(8,128)S(1)}, f32[128,2048]{1,0:T(8,128)S(1)}, u32[]{:S(2)}, u32[]{:S(2)}) collective-permute-start(f32[128,2048]{1,0:T(8,128)S(1)} %slice.236), channel_id=1, source_target_pairs={{0,2},{1,3},{2,0},{3,1},{4,6},{5,7},{6,4},{7,5},{8,10},{9,11},{10,... | collective-permute-start | bytes 3145736 | tf_op jit(solution)/shard_map/ppermute | solution.py:36
  867.1 44.7 %collective-permute-start.8 = (f32[128,2048]{1,0:T(8,128)S(1)}, f32[128,2048]{1,0:T(8,128)S(1)}, u32[]{:S(2)}, u32[]{:S(2)}) collective-permute-start(f32[128,2048]{1,0:T(8,128)S(1)} %fusion.74), channel_id=1, source_target_pairs={{0,2},{1,3},{2,0},{3,1},{4,6},{5,7},{6,4},{7,5},{8,10},{9,11},{10,... | collective-permute-start | bytes 3145736 | tf_op jit(solution)/shard_map/ppermute | solution.py:36
  890.9 42.9 %collective-permute-start.25 = (f32[128,2048]{1,0:T(8,128)S(1)}, f32[128,2048]{1,0:T(8,128)S(1)}, u32[]{:S(2)}, u32[]{:S(2)}) collective-permute-start(f32[128,2048]{1,0:T(8,128)S(1)} %add_reduce-precision_fusion), channel_id=1, source_target_pairs={{0,2},{1,3},{2,0},{3,1},{4,6},{5,7},{6,4},{7,5},{8,10},{9,11},{10,... | collective-permute-start | bytes 3145736 | tf_op jit(solution)/shard_map/ppermute | solution.py:36
  913.5 30.0 %collective-permute-start.9 = (f32[256,2048]{1,0:T(8,128)}, f32[256,2048]{1,0:T(8,128)}, u32[]{:S(2)}, u32[]{:S(2)}) collective-permute-start(f32[256,2048]{1,0:T(8,128)} %pad_maximum_fusion.4), channel_id=1, source_target_pairs={{0,1},{1,0},{2,3},{3,2},{4,5},{5,4},{6,7},{7,6},{8,9},{9,8},{10,11... | collective-permute-start | bytes 6291464 | tf_op jit(solution)/shard_map/ppermute | solution.py:36
  935.4 20.9 %collective-permute-start.26 = (f32[256,2048]{1,0:T(8,128)}, f32[256,2048]{1,0:T(8,128)}, u32[]{:S(2)}, u32[]{:S(2)}) collective-permute-start(f32[256,2048]{1,0:T(8,128)} %pad_maximum_fusion.9), channel_id=1, source_target_pairs={{0,1},{1,0},{2,3},{3,2},{4,5},{5,4},{6,7},{7,6},{8,9},{9,8},{10,11... | collective-permute-start | bytes 6291464 | tf_op jit(solution)/shard_map/ppermute | solution.py:36
  (109 other events, 1766.1 us)
Sparse Core Ops, SparseCore 0:
  258.6 83.0 reduce-scatter.10
  388.6 150.8 reduce-scatter.8
  580.3 165.8 reduce-scatter.6
  824.2 143.0 reduce-scatter.4
